TPU v7x, 512 devices: a whole 4x4x16 slice. The times are simulated.
512 devices in a mesh: row: 16 (over z), col: 4 (over x), depth: 8 (over y, core).
Axes of the slice: x: 4, y: 4, z: 16, core: 2. Of those that a mesh axis runs over, the one named last changes fastest.
Arguments:
- tokens: bfloat16 [1024, 4608], P(('row', 'depth'), 'col'), may hold values from -6 to 6
- grad_out: bfloat16 [1024, 4608], P(('row', 'depth'), 'col'), may hold values from -6 to 6
- w_gate: bfloat16 [18432, 4608], P(('row', 'depth'), 'col'), may hold values from -0.09375 to 0.09375
- w_up: bfloat16 [18432, 4608], P(('row', 'depth'), 'col'), may hold values from -0.09375 to 0.09375
- w_down: bfloat16 [18432, 4608], P(('row', 'depth'), 'col'), may hold values from -0.046875 to 0.046875
Outputs:
- grad_in: bfloat16 [1024, 4608], P(('row', 'depth'), 'col')
- grad_gate_w: float32 [18432, 4608], P(('row', 'depth'), 'col')
- grad_up_w: float32 [18432, 4608], P(('row', 'depth'), 'col')
- grad_down_w: float32 [18432, 4608], P(('row', 'depth'), 'col')
- grad_rms: float32 [3], replicated
All inputs are finite; a program needn't handle non-finite values.
Results may differ from a plain program's by a relative error of at most 0.0049.
Values may be sent and summed in bfloat16 or wider, within the bound.
A program may use at most 64 MiB of HBM per device.

v0:
```python
import jax
import jax.numpy as jnp
from jax import lax
from jax.sharding import Mesh
from jax.sharding import PartitionSpec as P

D = 4608
FF = 18432
DEPTH = ("depth_0", "depth_1")
ROW_COL_DEPTH = ("row", "col", "depth_0", "depth_1")
ROW_DEPTH = ("row", "depth_0", "depth_1")


tanh_scale = 0.7978845608028654
cubic_coeff = 0.044715


def sent_together(arrays, axis, dim, along):
    ends, at = ([], 0)
    for a in arrays[:-1]:
        at += a.shape[along]
        ends.append(at)
    both = jnp.concatenate(arrays, axis=along)
    return tuple(jnp.split(lax.all_gather(both, axis, axis=dim, tiled=True), ends, axis=along))


def split_up(value, dim, devices):
    dims = value.shape
    tiles = value.reshape(*dims[:dim], devices, dims[dim] // devices, *dims[dim + 1 :])
    return jnp.moveaxis(tiles, dim, 0)


def sent_and_summed(value, axis, dim):
    tiles = split_up(value, dim, lax.axis_size(axis))
    arrived = lax.all_to_all(tiles, axis, split_axis=0, concat_axis=0, tiled=True)
    return arrived.sum(axis=0)


def sent_together_2(arrays, axis, dim, along):
    ends, at = ([], 0)
    for a in arrays[:-1]:
        at += a.shape[along]
        ends.append(at)
    both = jnp.concatenate(arrays, axis=along)
    return tuple(jnp.split(sent_and_summed(both, axis, dim), ends, axis=along))


def rows_first(arrays, axis, dims):
    turned = [jnp.moveaxis(a, dim, 0) for a, dim in zip(arrays, dims)]
    both = jnp.concatenate([t.reshape(len(t), -1) for t in turned], axis=1)
    out, at, finished = (lax.all_gather(both, axis, axis=0, tiled=True), 0, [])
    for t, dim in zip(turned, dims):
        slab = out[:, at : at + t[0].size].reshape(-1, *t.shape[1:])
        finished.append(jnp.moveaxis(slab, 0, dim))
        at += t[0].size
    return tuple(finished)


def one_axis_at_a_time(value, axes):
    for axis in axes:
        value = lax.psum(value, axis)
    return value


def gelu_parts(pre_act):
    inner_arg = tanh_scale * (pre_act + cubic_coeff * pre_act * pre_act * pre_act)
    tanh_value = jnp.tanh(inner_arg)
    gelu_value = 0.5 * pre_act * (1.0 + tanh_value)
    gelu_slope = 0.5 * (1.0 + tanh_value) + 0.5 * pre_act * (
        1.0 - tanh_value * tanh_value
    ) * tanh_scale * (1.0 + 3.0 * cubic_coeff * pre_act * pre_act)
    return (gelu_value, gelu_slope)


def geglu_backward(gate_pre, up_pre, grad_hidden):
    gelu_value, gelu_slope = gelu_parts(gate_pre)
    hidden = (gelu_value * up_pre).astype(jnp.bfloat16)
    grad_gate = (grad_hidden * up_pre * gelu_slope).astype(jnp.bfloat16)
    grad_up = (grad_hidden * gelu_value).astype(jnp.bfloat16)
    return (hidden, grad_gate, grad_up)


def dot_transposed(left_side, right_side):
    return lax.dot_general(
        left_side, right_side, (((1,), (1,)), ((), ())), preferred_element_type=jnp.float32
    )


def sum_over_rows(left_side, right_side):
    return lax.dot_general(
        left_side, right_side, (((0,), (0,)), ((), ())), preferred_element_type=jnp.float32
    )


def body(tokens, grad_out, w_gate, w_up, w_down):
    group_x, group_dy = sent_together((tokens, grad_out), "row", 0, 1)
    gate_block, up_block, down_block = sent_together((w_gate, w_up, w_down), DEPTH, 0, 1)
    gate_part = dot_transposed(group_x, gate_block)
    up_part = dot_transposed(group_x, up_block)
    hidden_part = dot_transposed(group_dy, down_block)
    gate_share, up_share, hidden_share = sent_together_2(
        (gate_part, up_part, hidden_part), "col", 1, 0
    )
    hidden_piece, gate_piece, up_piece = geglu_backward(gate_share, up_share, hidden_share)
    hidden, grad_gate, grad_up = rows_first((hidden_piece, gate_piece, up_piece), "col", (1, 1, 1))
    input_part = jnp.dot(grad_gate, gate_block, preferred_element_type=jnp.float32) + jnp.dot(
        grad_up, up_block, preferred_element_type=jnp.float32
    )
    input_total = sent_and_summed(input_part, "row", 0)
    moved_hidden, moved_gate, moved_up = (
        lax.all_to_all(hidden, DEPTH, split_axis=1, concat_axis=0, tiled=True),
        lax.all_to_all(grad_gate, DEPTH, split_axis=1, concat_axis=0, tiled=True),
        lax.all_to_all(grad_up, DEPTH, split_axis=1, concat_axis=0, tiled=True),
    )
    every_x, every_dy = sent_together((group_x, group_dy), DEPTH, 0, 1)
    grad_gate_w = sum_over_rows(moved_gate, every_x)
    grad_up_w = sum_over_rows(moved_up, every_x)
    grad_down_w = sum_over_rows(moved_hidden, every_dy)
    grad_in = input_total.astype(jnp.bfloat16)
    gate_sq, up_sq, down_sq = (
        one_axis_at_a_time(jnp.sum(grad_gate_w * grad_gate_w), ROW_COL_DEPTH),
        one_axis_at_a_time(jnp.sum(grad_up_w * grad_up_w), ROW_COL_DEPTH),
        one_axis_at_a_time(jnp.sum(grad_down_w * grad_down_w), ROW_COL_DEPTH),
    )
    entries = jnp.float32(D * FF)
    grad_rms = jnp.stack(
        [jnp.sqrt(gate_sq / entries), jnp.sqrt(up_sq / entries), jnp.sqrt(down_sq / entries)]
    )
    return (grad_in, grad_gate_w, grad_up_w, grad_down_w, grad_rms)


def solution(mesh):
    torus = Mesh(
        mesh.devices.reshape(mesh.shape["row"], mesh.shape["col"], 4, 2),
        ("row", "col", "depth_0", "depth_1"),
    )
    placed = (
        P(ROW_DEPTH, "col"),
        P(ROW_DEPTH, "col"),
        P(ROW_DEPTH, "col"),
        P(ROW_DEPTH, "col"),
        P(ROW_DEPTH, "col"),
    )
    return jax.shard_map(
        body,
        mesh=torus,
        in_specs=placed,
        out_specs=(
            P(ROW_DEPTH, "col"),
            P(ROW_DEPTH, "col"),
            P(ROW_DEPTH, "col"),
            P(ROW_DEPTH, "col"),
            P(),
        ),
        check_vma=False,
    )
```

profile of v0, /device:TPU:1, one launch (start us, length us, event | category | flops | bytes accessed | tf_op | source)
XLA Modules:
  0.0 253.0 jit_solution(7441306466861003992)
XLA Ops:
  7.2 0.0 copy-start.1
  7.2 0.0 copy-start.2
  7.2 0.0 all-gather.3.cloned.1.call-start
  7.2 2.3 pad_maximum_fusion.1
  9.5 0.0 all-gather.3.cloned.1.call-update
  9.5 0.0 all-gather.5.cloned.1.call-start
  9.6 0.0 copy-done.1
  9.6 0.0 copy-done.2
  9.6 35.9 %all_gather.12 = bf16[128,2304]{1,0:T(8,128)(2,1)} all-gather(bf16[8,2304]{1,0:T(8,128)(2,1)S(1)} %pad_maximum_fusion.3), channel_id=1, replica_groups=mesh['row'=16,'col'=4,'depth_0'=4,'depth_1'=2] {'row'}, dimensions={0}, use_global_device_ids=true | all-gather | bytes 626688 | tf_op jit(solution)/shard_map/all_gather | solution.py:24
  45.5 0.0 copy-start
  45.5 0.0 all-gather.5.cloned.1.call-update
  45.5 25.9 %all-gather.3.cloned.1.call-done = bf16[1152,3456]{1,0:T(8,128)(2,1)} async-done(((bf16[144,3456]{1,0:T(8,128)(2,1)}), bf16[1152,3456]{1,0:T(8,128)(2,1)}) %all-gather.3.cloned.1.call-update) | async-done | bytes 7962640 | tf_op jit(solution)/shard_map/all_gather | solution.py:24
  71.4 2.8 %fusion = f32[128,1152]{1,0:T(8,128)S(1)} fusion(bf16[1152,3456]{1,0:T(8,128)(2,1)} %all-gather.3.cloned.1.call-done, bf16[128,2304]{1,0:T(8,128)(2,1)} %all_gather.12), kind=kOutput, calls=%fused_computation | convolution fusion | flops 339738624 | bytes 3538944 | tf_op jit(solution)/shard_map/dot_general | solution.py:84
  74.2 0.0 copy-done
  74.2 2.7 %fusion.6 = f32[128,1152]{1,0:T(8,128)S(1)} fusion(bf16[1152,3456]{1,0:T(8,128)(2,1)} %all-gather.3.cloned.1.call-done, bf16[128,2304]{1,0:T(8,128)(2,1)S(1)} %copy-done), kind=kOutput, calls=%fused_computation.7 | convolution fusion | flops 339738624 | bytes 3538944 | tf_op jit(solution)/shard_map/dot_general | solution.py:84
  76.9 2.7 %fusion.10 = f32[128,1152]{1,0:T(8,128)S(1)} fusion(bf16[1152,3456]{1,0:T(8,128)(2,1)} %all-gather.3.cloned.1.call-done, bf16[128,2304]{1,0:T(8,128)(2,1)S(1)} %copy-done), kind=kOutput, calls=%fused_computation.11 | convolution fusion | flops 339738624 | bytes 3538944 | tf_op jit(solution)/shard_map/dot_general | solution.py:84
  79.5 0.1 pad_maximum_fusion
  79.7 1.2 copy.10
  80.9 26.0 %all_to_all.67 = f32[4,384,288]{1,2,0:T(8,128)S(1)} all-to-all(f32[4,384,288]{1,2,0:T(8,128)S(1)} %bitcast.53), channel_id=1, replica_groups=mesh['row'=16,'col'=4,'depth_0'=4,'depth_1'=2] {'col'}, dimensions={0} | all-to-all | bytes 3538944 | tf_op jit(solution)/shard_map/all_to_all | solution.py:35
  106.9 0.1 reduce_sum.45
  107.0 0.1 fusion.32
  107.2 11.6 %all_gather.14 = bf16[1152,384]{1,0:T(8,128)(2,1)S(1)} all-gather(bf16[288,384]{1,0:T(8,128)(2,1)S(1)} %pad_maximum_fusion.2), channel_id=1, replica_groups=mesh['row'=16,'col'=4,'depth_0'=4,'depth_1'=2] {'col'}, dimensions={0}, use_global_device_ids=true | all-gather | bytes 1105920 | tf_op jit(solution)/shard_map/all_gather | solution.py:51
  118.8 1.0 fusion.37
  119.8 14.7 %all_to_all.68 = bf16[128,8,144]{0,2,1:T(8,128)(2,1)S(1)} all-to-all(bf16[128,8,144]{0,2,1:T(8,128)(2,1)S(1)} %bitcast.54), channel_id=1, replica_groups=mesh['row'=16,'col'=4,'depth_0'=4,'depth_1'=2] {'depth_0','depth_1'}, dimensions={1} | all-to-all | bytes 589824 | tf_op jit(solution)/shard_map/all_to_all | solution.py:112
  134.5 3.9 %all-to-all-start.3 = ((bf16[128,8,144]{0,2,1:T(8,128)(2,1)}), bf16[128,8,144]{0,2,1:T(8,128)(2,1)S(1)}, u32[]{:S(2)}, u32[]{:S(2)}) async-start(bf16[128,8,144]{0,2,1:T(8,128)(2,1)} %bitcast.10), calls=%async_computation.3 | async-start | bytes 589824 | tf_op jit(solution)/shard_map/all_to_all | solution.py:113
  138.4 2.4 fusion.8
  140.7 4.4 %all-to-all-done.3 = bf16[128,8,144]{0,2,1:T(8,128)(2,1)S(1)} async-done(((bf16[128,8,144]{0,2,1:T(8,128)(2,1)}), bf16[128,8,144]{0,2,1:T(8,128)(2,1)S(1)}, u32[]{:S(2)}, u32[]{:S(2)}) %all-to-all-start.3) | async-done | bytes 294944 | tf_op jit(solution)/shard_map/all_to_all | solution.py:113
  145.2 4.4 %all-to-all-start.4 = ((bf16[128,8,144]{0,2,1:T(8,128)(2,1)}), bf16[128,8,144]{0,2,1:T(8,128)(2,1)S(1)}, u32[]{:S(2)}, u32[]{:S(2)}) async-start(bf16[128,8,144]{0,2,1:T(8,128)(2,1)} %bitcast.13), calls=%async_computation.4 | async-start | bytes 589824 | tf_op jit(solution)/shard_map/all_to_all | solution.py:111
  149.6 3.2 %fusion.2 = f32[16,8,1152]{2,1,0:T(8,128)} fusion(f32[128,1152]{1,0:T(8,128)S(1)} %fusion.8, bf16[1152,3456]{1,0:T(8,128)(2,1)} %all-gather.3.cloned.1.call-done, bf16[1152,384]{1,0:T(8,128)(2,1)S(1)} %all_gather.14), kind=kOutput, calls=%fused_computation.3 | convolution fusion | flops 339886080 | bytes 4128768 | tf_op jit(solution)/shard_map/dot_general | solution.py:106
  152.8 3.6 %all-to-all-done.4 = bf16[128,8,144]{0,2,1:T(8,128)(2,1)S(1)} async-done(((bf16[128,8,144]{0,2,1:T(8,128)(2,1)}), bf16[128,8,144]{0,2,1:T(8,128)(2,1)S(1)}, u32[]{:S(2)}, u32[]{:S(2)}) %all-to-all-start.4) | async-done | bytes 294944 | tf_op jit(solution)/shard_map/all_to_all | solution.py:111
  156.4 12.0 %all-to-all-start.1 = ((f32[16,8,1152]{2,1,0:T(8,128)}), f32[16,8,1152]{2,1,0:T(8,128)S(1)}, u32[]{:S(2)}, u32[]{:S(2)}) async-start(f32[16,8,1152]{2,1,0:T(8,128)} %fusion.2), calls=%async_computation.1 | async-start | bytes 1179648 | tf_op jit(solution)/shard_map/all_to_all | solution.py:35
  168.4 0.0 all-gather.5.cloned.1.call-done
  168.5 0.0 copy-start.3
  168.5 3.8 %multiply_reduce_fusion.2 = (f32[]{:T(128)}, f32[144,1152]{1,0:T(8,128)}) fusion(bf16[1024,2304]{1,0:T(8,128)(2,1)} %all-gather.5.cloned.1.call-done, bf16[128,8,144]{0,2,1:T(8,128)(2,1)S(1)} %all_to_all.68), kind=kOutput, calls=%fused_computation.21 | convolution fusion | flops 340070400 | bytes 3317764 | tf_op jit(solution)/shard_map/dot_general | solution.py:90
  172.3 3.7 %multiply_reduce_fusion.1 = (f32[]{:T(128)}, f32[144,1152]{1,0:T(8,128)}) fusion(bf16[1024,2304]{1,0:T(8,128)(2,1)} %all-gather.5.cloned.1.call-done, bf16[128,8,144]{0,2,1:T(8,128)(2,1)S(1)} %all-to-all-done.3), kind=kOutput, calls=%fused_computation.20 | convolution fusion | flops 340070400 | bytes 3317764 | tf_op jit(solution)/shard_map/dot_general | solution.py:90
  175.9 0.0 copy-done.3
  175.9 2.0 multiply_reduce_fusion
  177.9 36.3 %all-reduce = (f32[]{:T(128)}, f32[]{:T(128)}, f32[]{:T(128)}) all-reduce(f32[]{:T(128)} %get-tuple-element.23, f32[]{:T(128)} %get-tuple-element.25, f32[]{:T(128)} %get-tuple-element.27), channel_id=1, replica_groups=mesh['row'=16,'col'=4,'depth_0'=4,'depth_1'=2] {'row'}, use_global_device_ids=true, to_apply=%region_13.0 | all-reduce | flops 3 | bytes 24 | tf_op jit(solution)/shard_map/psum | solution.py:61
  214.2 7.2 %all-reduce.2 = (f32[]{:T(128)}, f32[]{:T(128)}, f32[]{:T(128)}) all-reduce(f32[]{:T(128)} %get-tuple-element.5, f32[]{:T(128)} %get-tuple-element.6, f32[]{:T(128)} %get-tuple-element.7), channel_id=1, replica_groups=mesh['row'=16,'col'=4,'depth_0'=4,'depth_1'=2] {'col'}, use_global_device_ids=true, to_apply=%region_14.0 | all-reduce | flops 3 | bytes 24 | tf_op jit(solution)/shard_map/psum | solution.py:61
  221.4 7.6 %all-reduce.1 = (f32[]{:T(128)}, f32[]{:T(128)}, f32[]{:T(128)}) all-reduce(f32[]{:T(128)} %get-tuple-element.11, f32[]{:T(128)} %get-tuple-element.12, f32[]{:T(128)} %get-tuple-element.13), channel_id=1, replica_groups=mesh['row'=16,'col'=4,'depth_0'=4,'depth_1'=2] {'depth_0'}, use_global_device_ids=true, to_apply=%region_15.0 | all-reduce | flops 3 | bytes 24 | tf_op jit(solution)/shard_map/psum | solution.py:61
  229.0 14.0 %all-reduce.3 = (f32[]{:T(128)}, f32[]{:T(128)}, f32[]{:T(128)}) all-reduce(f32[]{:T(128)} %get-tuple-element.8, f32[]{:T(128)} %get-tuple-element.9, f32[]{:T(128)} %get-tuple-element.10), channel_id=1, replica_groups=mesh['row'=16,'col'=4,'depth_0'=4,'depth_1'=2] {'depth_1'}, use_global_device_ids=true, to_apply=%region_16.0 | all-reduce | flops 3 | bytes 24 | tf_op jit(solution)/shard_map/psum | solution.py:61
  244.9 0.6 pad_maximum_fusion.4
  245.5 0.0 all-to-all-done.1
  245.5 0.6 reduce_sum.46
  (2 shorter events, 0.0 us)
Async XLA Ops:
  7.2 2.4 copy-start.1
  7.2 2.4 copy-start.2
  7.2 64.2 %all-gather.3.cloned.1.call-start = ((), (), s32[]{:S(2)}) async-start(), calls=%async_computation.5 | async-start | bytes 8957952 | tf_op jit(solution)/shard_map/all_gather | solution.py:24
  9.5 158.9 %all-gather.5.cloned.1.call-start = ((), (), s32[]{:S(2)}) async-start(), calls=%async_computation.6 | async-start | bytes 5308416 | tf_op jit(solution)/shard_map/all_gather | solution.py:24
  45.5 28.7 %copy-start = (bf16[128,2304]{1,0:T(8,128)(2,1)S(1)}, bf16[128,2304]{1,0:T(8,128)(2,1)}, u32[]{:S(2)}) copy-start(bf16[128,2304]{1,0:T(8,128)(2,1)} %all_gather.12) | copy-start | bytes 1769476
  134.5 10.7 %all-to-all-start.3 = ((bf16[128,8,144]{0,2,1:T(8,128)(2,1)}), bf16[128,8,144]{0,2,1:T(8,128)(2,1)S(1)}, u32[]{:S(2)}, u32[]{:S(2)}) async-start(bf16[128,8,144]{0,2,1:T(8,128)(2,1)} %bitcast.10), calls=%async_computation.3 | async-start | bytes 589824 | tf_op jit(solution)/shard_map/all_to_all | solution.py:113
  145.2 11.2 %all-to-all-start.4 = ((bf16[128,8,144]{0,2,1:T(8,128)(2,1)}), bf16[128,8,144]{0,2,1:T(8,128)(2,1)S(1)}, u32[]{:S(2)}, u32[]{:S(2)}) async-start(bf16[128,8,144]{0,2,1:T(8,128)(2,1)} %bitcast.13), calls=%async_computation.4 | async-start | bytes 589824 | tf_op jit(solution)/shard_map/all_to_all | solution.py:111
  156.4 89.1 %all-to-all-start.1 = ((f32[16,8,1152]{2,1,0:T(8,128)}), f32[16,8,1152]{2,1,0:T(8,128)S(1)}, u32[]{:S(2)}, u32[]{:S(2)}) async-start(f32[16,8,1152]{2,1,0:T(8,128)} %fusion.2), calls=%async_computation.1 | async-start | bytes 1179648 | tf_op jit(solution)/shard_map/all_to_all | solution.py:35
  168.5 7.5 %copy-start.3 = (bf16[1024,2304]{1,0:T(8,128)(2,1)S(1)}, bf16[1024,2304]{1,0:T(8,128)(2,1)}, u32[]{:S(2)}) copy-start(bf16[1024,2304]{1,0:T(8,128)(2,1)} %all-gather.5.cloned.1.call-done) | copy-start | bytes 14155780
Sparse Core Ops, SparseCore 0:
  10.1 61.2 all-gather.2
  73.5 42.1 all-gather.4
where the time goes:
time: 254 us; the launch traced here: 253 us
  blocking collectives  153 us (60%)
  waiting for transfers between devices  34 us (13%)
  matrix products  23.1 us (9%)
  starting transfers between devices  20.4 us (8%)
  between operations  16.2 us (6%)
  other arithmetic  3.92 us (2%)
    psum x4, blocking collectives, one_axis_at_a_time(): value = lax.psum(value, axis)  65 us
    all_gather x1, blocking collectives, sent_together(): lax.all_gather(both, axis, axis=dim, tiled=True)  35.9 us
    all_to_all x1, blocking collectives, sent_and_summed(): lax.all_to_all(tiles, axis, split_axis=0, concat_axis=0, tiled=True)  26 us
    all_gather x2, waiting for transfers between devices, sent_together(): lax.all_gather(both, axis, axis=dim, tiled=True)  25.9 us
    all_to_all x1, blocking collectives, body(): lax.all_to_all(grad_gate, DEPTH, split_axis=1, concat_axis=0, tiled=True)  14.7 us
    all_to_all x1, starting transfers between devices, sent_and_summed(): lax.all_to_all(tiles, axis, split_axis=0, concat_axis=0, tiled=True)  12 us
    all_gather x1, blocking collectives, rows_first(): out, at, finished = (lax.all_gather(both, axis, axis=0, tiled=True), 0, [])  11.6 us
    dot_general x3, matrix products, sum_over_rows(): lax.dot_general(left_side, right_side, (((0,), (0,)), ((), ())), preferre...  9.47 us
  transfers between devices with their start and end apart: 5, of which 3 were waited for; matrix products, arithmetic and copies ran while one was open for 10% of the time, Pallas kernels for 0%

commit v1 on v0

v1 whole, which is shorter than its diff:
```python
import functools

import jax
import jax.numpy as jnp
from jax import lax
from jax.experimental import pallas as pl
from jax.experimental.pallas import tpu as pltpu
from jax.sharding import Mesh
from jax.sharding import PartitionSpec as P

D = 4608
FF = 18432
ROW_DEPTH = ("row", "depth_0", "depth_1")
Z, X, Y = 16, 4, 4
STEPS = Z // 2
F32 = jnp.float32
BF16 = jnp.bfloat16
MESH = pl.DeviceIdType.MESH

tanh_scale = 0.7978845608028654
cubic_coeff = 0.044715


def gelu_parts(pre_act):
    inner_arg = tanh_scale * (pre_act + cubic_coeff * pre_act * pre_act * pre_act)
    tanh_value = jnp.tanh(inner_arg)
    gelu_value = 0.5 * pre_act * (1.0 + tanh_value)
    gelu_slope = 0.5 * (1.0 + tanh_value) + 0.5 * pre_act * (
        1.0 - tanh_value * tanh_value
    ) * tanh_scale * (1.0 + 3.0 * cubic_coeff * pre_act * pre_act)
    return (gelu_value, gelu_slope)


def geglu_backward(gate_pre, up_pre, grad_hidden):
    gelu_value, gelu_slope = gelu_parts(gate_pre)
    return (
        gelu_value * up_pre,
        grad_hidden * up_pre * gelu_slope,
        grad_hidden * gelu_value,
    )


def nt(a, b):
    return lax.dot_general(a, b, (((1,), (1,)), ((), ())), preferred_element_type=F32)


def nn(a, b):
    return lax.dot_general(a, b, (((1,), (0,)), ((), ())), preferred_element_type=F32)


def tn(a, b):
    return lax.dot_general(a, b, (((0,), (0,)), ((), ())), preferred_element_type=F32)


def kernel(
    x_ref, dy_ref, wg_ref, wu_ref, wd_ref,
    gi_out, gw_out, uw_out, dw_out, rms_out,
    blk, wm, wlx, wld, pf, sx, rx, g, xs, gi, sy, ry, sz, rz, acc,
    wo, wp, wr, rb, sb,
    ysend, yrecv, wlocal, wsend, wrecv, fsend, frecv,
    xsend, xrecv, gsend, grecv, rysend, ryrecv, rzsend, rzrecv,
    psend, precv, osend, nsend, nrecv,
):
    z = lax.axis_index("row")
    x = lax.axis_index("col")
    y = lax.axis_index("depth_0")
    k = lax.axis_index("depth_1")
    other = 1 - k

    def zdev(o):
        return {"row": lax.rem(z + o, Z)}

    def xdev(o):
        return {"col": lax.rem(x + o, X)}

    def ydev(o):
        return {"depth_0": lax.rem(y + o, Y)}

    mate = {"depth_1": other}

    def rcopy(src, dst, s, r, dev):
        return pltpu.make_async_remote_copy(
            src_ref=src, dst_ref=dst, send_sem=s, recv_sem=r, device_id=dev, device_id_type=MESH
        )

    def wait_bytes(ref, sem):
        pltpu.make_async_copy(ref, ref, sem).wait()

    barrier = pltpu.get_barrier_semaphore()
    for o in range(1, Z):
        pl.semaphore_signal(barrier, inc=1, device_id=zdev(o), device_id_type=MESH)
    for o in range(1, X):
        pl.semaphore_signal(barrier, inc=1, device_id=xdev(o), device_id_type=MESH)
    for o in range(1, Y):
        pl.semaphore_signal(barrier, inc=1, device_id=ydev(o), device_id_type=MESH)
    pl.semaphore_signal(barrier, inc=1, device_id=mate, device_id_type=MESH)

    weights = (wg_ref, wu_ref, wd_ref)

    def tail_of(p):
        return (wlx, 0) if p == 0 else (wlx, 32) if p == 1 else (wld, 64)

    wlx[64:128, :] = jnp.zeros((64, wlx.shape[1]), BF16)
    wld[0:64, :] = jnp.zeros((64, wld.shape[1]), BF16)
    wld[96:128, :] = jnp.zeros((32, wld.shape[1]), BF16)
    local = []
    for p in range(3):
        tail, at = tail_of(p)
        local.append(
            pltpu.make_async_copy(weights[p].at[0:128], wm.at[p, 0:128], wlocal.at[2 * p])
        )
        local.append(
            pltpu.make_async_copy(
                weights[p].at[128:144], tail.at[at : at + 16], wlocal.at[2 * p + 1]
            )
        )
    for c in local:
        c.start()
    blk[0, 0, 0, pl.ds(y, 1)] = x_ref[...][None]
    blk[0, 0, 1, pl.ds(y, 1)] = dy_ref[...][None]

    pl.semaphore_wait(barrier, (Z - 1) + (X - 1) + (Y - 1) + 1)

    ycopies = []
    for xd, src in ((0, x_ref), (1, dy_ref)):
        for o in (1, 3, 2):
            c = rcopy(
                src, blk.at[0, 0, xd, y], ysend.at[xd, o - 1], yrecv.at[xd, o - 1], ydev(o)
            )
            c.start()
            ycopies.append(c)
    wcopies = []
    for p in range(3):
        tail, at = tail_of(p)
        wcopies.append(
            rcopy(
                weights[p].at[0:128], wm.at[p, 128:256], wsend.at[2 * p], wrecv.at[2 * p], mate
            )
        )
        wcopies.append(
            rcopy(
                weights[p].at[128:144],
                tail.at[at + 16 : at + 32],
                wsend.at[2 * p + 1],
                wrecv.at[2 * p + 1],
                mate,
            )
        )
    for c in wcopies:
        c.start()

    def ring(direction, src_dir, src_slot, dst_dir, dst_slot, xd, sem_slot):
        return rcopy(
            blk.at[src_dir, src_slot, xd],
            blk.at[dst_dir, dst_slot, xd],
            fsend.at[direction, sem_slot, xd],
            frecv.at[dst_dir, dst_slot, xd],
            zdev(1) if direction == 0 else zdev(Z - 1),
        )

    for xd in range(2):
        for o in range(1, Y):
            ycopies[3 * xd + o - 1].wait_recv()
        ring(0, 0, 0, 0, 1, xd, 0).start()
        ring(1, 0, 0, 1, 1, xd, 0).start()

    for c in local:
        c.wait()
    for c in wcopies:
        c.wait_recv()

    def got(direction, slot, xd):
        wait_bytes(blk.at[direction, slot, xd], frecv.at[direction, slot, xd])

    def stage_a(t):
        @pl.when(t < STEPS)
        def _():
            for xd in range(2):
                for direction in range(2):
                    got(direction, t, xd)

                    @pl.when(t < STEPS - 1)
                    def _():
                        ring(direction, direction, t, direction, t + 1, xd, t).start()

                    if direction == xd:

                        @pl.when(t == STEPS - 1)
                        def _():
                            ring(direction, direction, t, 1, 0, xd, t).start()

        @pl.when(t == STEPS)
        def _():
            got(1, 0, 0)
            got(1, 0, 1)

        slot = lax.rem(t, STEPS)
        it = t - 1
        xv = blk[:, pl.ds(slot, 1), 0].astype(F32).reshape(64, -1).astype(BF16)
        dv = blk[:, pl.ds(slot, 1), 1].astype(F32).reshape(64, -1).astype(BF16)
        xs[0, pl.ds(it, 1)] = xv[None]
        xs[1, pl.ds(it, 1)] = dv[None]
        parts = (
            (nt(xv, wm[0]), 0),
            (nt(xv, wm[1]), 256),
            (nt(dv, wm[2]), 512),
            (nt(xv, wlx[...]) + nt(dv, wld[...]), 768),
        )
        for value, at in parts:
            pf[pl.ds(it, 1), :, :, at : at + value.shape[1]] = value.reshape(1, X, 16, -1)
        for o in (2, 1, 3):
            j = lax.rem(x + o, X)
            sx[it, o - 1] = pf[it, j].astype(BF16)
            rcopy(
                sx.at[it, o - 1], rx.at[it, o - 1], xsend.at[it], xrecv.at[it], xdev(o)
            ).start()

    lane = lax.broadcasted_iota(jnp.int32, (16, 128), 1)

    def stage_b(i):
        wait_bytes(rx.at[i], xrecv.at[i])
        total = pf[i, x]
        for o in range(3):
            total = total + rx[i, o].astype(F32)
        hid, gg, gu = geglu_backward(total[:, 0:256], total[:, 256:512], total[:, 512:768])
        left = total[:, 768:896]
        hid_l, gg_l, gu_l = geglu_backward(
            left, pltpu.roll(left, 96, 1), pltpu.roll(left, 64, 1)
        )
        packed = jnp.where(
            lane < 32,
            gg_l,
            jnp.where(
                lane < 64,
                pltpu.roll(gu_l, 32, 1),
                jnp.where(lane < 96, pltpu.roll(hid_l, 64, 1), 0.0),
            ),
        )
        g[i, x, :, 0:256] = gg.astype(BF16)
        g[i, x, :, 256:512] = gu.astype(BF16)
        g[i, x, :, 512:768] = hid.astype(BF16)
        g[i, x, :, 768:896] = packed.astype(BF16)
        for o in (2, 1, 3):
            rcopy(g.at[i, x], g.at[i, x], gsend.at[i], grecv.at[i], xdev(o)).start()

    def stage_c(i):
        wait_bytes(g.at[i, 0:3], grecv.at[i])
        gv = g[i].reshape(64, 896)
        part = (
            nn(gv[:, 0:256], wm[0]) + nn(gv[:, 256:512], wm[1]) + nn(gv[:, 768:896], wlx[...])
        )
        gi[pl.ds(i, 1)] = part.reshape(1, 2, Y, 8, -1)
        for o in (2, 1, 3):
            j = lax.rem(y + o, Y)
            sy[i, o - 1] = gi[i, :, j].astype(BF16)
            rcopy(
                sy.at[i, o - 1], ry.at[i, o - 1], rysend.at[i], ryrecv.at[i], ydev(o)
            ).start()

    def stage_d(i):
        wait_bytes(ry.at[i], ryrecv.at[i])
        total = gi[i, :, y]
        for o in range(3):
            total = total + ry[i, o].astype(F32)
        sz[i] = total.astype(BF16)
        t = i + 1

        @pl.when(t < STEPS)
        def _():
            rcopy(
                sz.at[i, 0], rz.at[t - 1], rzsend.at[i, 0], rzrecv, zdev(Z - t)
            ).start()

        @pl.when(t == STEPS)
        def _():
            acc[...] = total[0]

        rcopy(
            sz.at[i, 1], rz.at[STEPS - 2 + t], rzsend.at[i, 1], rzrecv, zdev(t)
        ).start()

    def step(t, carry):
        pl.when(t <= STEPS)(lambda: stage_a(t))
        pl.when((t >= 2) & (t <= STEPS + 1))(lambda: stage_b(t - 2))
        pl.when((t >= 3) & (t <= STEPS + 2))(lambda: stage_c(t - 3))
        pl.when(t >= 4)(lambda: stage_d(t - 4))
        return carry

    lax.fori_loop(1, STEPS + 3, step, 0)

    tokens = STEPS * 64
    gall = g[...].reshape(tokens, 896)
    xall = xs[0].reshape(tokens, -1)
    dall = xs[1].reshape(tokens, -1)
    tail_x = tn(gall[:, 768:896], xall)
    tail_d = tn(gall[:, 768:896], dall)
    tails = (tail_x[0:32], tail_x[32:64], tail_d[64:96])
    pcopies = []
    for p, right in ((0, xall), (1, xall), (2, dall)):
        main = tn(gall[:, 256 * p : 256 * p + 256], right)
        wp[p, 0:128] = main[128:256]
        wp[p, 128:144] = tails[p][16:32]
        c = rcopy(wp.at[p], wr.at[p], psend.at[p], precv.at[p], mate)
        c.start()
        pcopies.append(c)
        wo[p, 0:128] = main[0:128]
        wo[p, 128:144] = tails[p][0:16]

    stage_d(STEPS - 1)

    outs = (gw_out, uw_out, dw_out)
    ocopies = []
    squares = []
    for p in range(3):
        pcopies[p].wait_recv()
        total = wo[p] + wr[p]
        wo[p] = total
        c = pltpu.make_async_copy(wo.at[p], outs[p], osend.at[p])
        c.start()
        ocopies.append(c)
        squares.append(jnp.sum((total * total).reshape(18, 8, -1), axis=0))
    lanes = lax.broadcasted_iota(jnp.int32, (8, 128), 1)
    value = jnp.zeros((8, 128), F32)
    for p in range(3):
        value = jnp.where(lanes == p, jnp.sum(squares[p]), value)

    ncopies = []

    def norm_stage(stage, value, count, me, dev):
        sb[stage] = value
        rb[stage, me] = value
        for o in range(1, count):
            rcopy(
                sb.at[stage], rb.at[stage, me], nsend.at[stage], nrecv.at[stage], dev(o)
            ).start()
        wait_bytes(rb.at[stage, 0 : count - 1], nrecv.at[stage])
        total = rb[stage, 0]
        for j in range(1, count):
            total = total + rb[stage, j]
        return total

    value = norm_stage(0, value, 2, k, lambda o: mate)
    value = norm_stage(1, value, X, x, xdev)
    value = norm_stage(2, value, Y, y, ydev)
    value = norm_stage(3, value, Z, z, zdev)
    rms_out[...] = jnp.sqrt(value / F32(D * FF))

    wait_bytes(rz, rzrecv)
    total = acc[...]
    for j in range(Z - 1):
        total = total + rz[j].astype(F32)
    gi_out[...] = total.astype(BF16)

    for c in ycopies:
        c.wait_send()
    for c in wcopies:
        c.wait_send()
    for s in range(STEPS):
        for xd in range(2):
            for direction in range(2):
                if s < STEPS - 1 or direction == xd:
                    wait_bytes(blk.at[direction, 0, xd], fsend.at[direction, s, xd])
        wait_bytes(sx.at[s], xsend.at[s])
        wait_bytes(g.at[s, 0:3], gsend.at[s])
        wait_bytes(sy.at[s], rysend.at[s])
        if s < STEPS - 1:
            wait_bytes(sz.at[s, 0], rzsend.at[s, 0])
        wait_bytes(sz.at[s, 1], rzsend.at[s, 1])
    for c in pcopies:
        c.wait_send()
    for c in ocopies:
        c.wait()
    for stage, count in enumerate((2, X, Y, Z)):
        wait_bytes(rb.at[stage, 0 : count - 1], nsend.at[stage])


def body(tokens, grad_out, w_gate, w_up, w_down):
    c = tokens.shape[1]
    h = w_gate.shape[0]
    vmem = pl.BlockSpec(memory_space=pltpu.VMEM)
    hbm = pl.BlockSpec(memory_space=pl.ANY)
    dma = pltpu.SemaphoreType.DMA
    wgrad = jax.ShapeDtypeStruct((h, c), F32)
    grad_in, gw, uw, dw, rms = pl.pallas_call(
        kernel,
        out_shape=(
            jax.ShapeDtypeStruct(tokens.shape, BF16),
            wgrad,
            wgrad,
            wgrad,
            jax.ShapeDtypeStruct((8, 128), F32),
        ),
        in_specs=[vmem, vmem, hbm, hbm, hbm],
        out_specs=(vmem, hbm, hbm, hbm, vmem),
        scratch_shapes=[
            pltpu.VMEM((2, STEPS, 2, Y, 8, c), BF16),
            pltpu.VMEM((3, 256, c), BF16),
            pltpu.VMEM((128, c), BF16),
            pltpu.VMEM((128, c), BF16),
            pltpu.VMEM((STEPS, X, 16, 896), F32),
            pltpu.VMEM((STEPS, 3, 16, 896), BF16),
            pltpu.VMEM((STEPS, 3, 16, 896), BF16),
            pltpu.VMEM((STEPS, X, 16, 896), BF16),
            pltpu.VMEM((2, STEPS, 64, c), BF16),
            pltpu.VMEM((STEPS, 2, Y, 8, c), F32),
            pltpu.VMEM((STEPS, 3, 2, 8, c), BF16),
            pltpu.VMEM((STEPS, 3, 2, 8, c), BF16),
            pltpu.VMEM((STEPS, 2, 8, c), BF16),
            pltpu.VMEM((Z - 1, 8, c), BF16),
            pltpu.VMEM((8, c), F32),
            pltpu.VMEM((3, h, c), F32),
            pltpu.VMEM((3, h, c), F32),
            pltpu.VMEM((3, h, c), F32),
            pltpu.VMEM((4, Z, 8, 128), F32),
            pltpu.VMEM((4, 8, 128), F32),
            dma((2, 3)), dma((2, 3)), dma((6,)), dma((6,)), dma((6,)),
            dma((2, STEPS, 2)), dma((2, STEPS, 2)),
            dma((STEPS,)), dma((STEPS,)), dma((STEPS,)), dma((STEPS,)),
            dma((STEPS,)), dma((STEPS,)), dma((STEPS, 2)), dma,
            dma((3,)), dma((3,)), dma((3,)), dma((4,)), dma((4,)),
        ],
        compiler_params=pltpu.CompilerParams(
            collective_id=0, has_side_effects=True, vmem_limit_bytes=60 * 1024 * 1024
        ),
    )(tokens, grad_out, w_gate, w_up, w_down)
    return (grad_in, gw, uw, dw, rms[0, 0:3])


def solution(mesh):
    torus = Mesh(
        mesh.devices.reshape(mesh.shape["row"], mesh.shape["col"], 4, 2),
        ("row", "col", "depth_0", "depth_1"),
    )
    placed = P(ROW_DEPTH, "col")
    return jax.shard_map(
        body,
        mesh=torus,
        in_specs=(placed,) * 5,
        out_specs=(placed, placed, placed, placed, P()),
        check_vma=False,
    )
```

time: 254 us -> 94.1 us (0.37)
  blocking collectives: 153 us -> 0 us
  Pallas kernels: 0 us -> 85.3 us
  waiting for transfers between devices: 34 us -> 0 us
  matrix products: 23.1 us -> 0 us
  starting transfers between devices: 20.4 us -> 0 us
  between operations: 16.2 us -> 0.64 us
  local copies, waits for them, and re-layouts: 2.16 us -> 6.73 us
  other arithmetic: 3.92 us -> 0 us
    pallas_call x0 -> x1, Pallas kernels: none -> 85.3 us  [body(): pl.pallas_call(kernel, out_shape=(jax.ShapeDtypeStruct(tokens.shape, BF16...]
    psum x4 -> x0, blocking collectives: 65 us -> none  [one_axis_at_a_time(): value = lax.psum(value, axis)]
    all_gather x2 -> x0, blocking collectives: 47.5 us -> none  [the longest x1 35.9 us: sent_together(): lax.all_gather(both, axis, axis=dim, tiled=True)]
    all_to_all x2 -> x0, blocking collectives: 40.8 us -> none  [the longest x1 26 us: sent_and_summed(): lax.all_to_all(tiles, axis, split_axis=0, concat_axis=0, tiled=True)]
    all_gather x2 -> x0, waiting for transfers between devices: 25.9 us -> none  [sent_together(): lax.all_gather(both, axis, axis=dim, tiled=True)]
    dot_general x8 -> x0, matrix products: 23.1 us -> none  [the longest x3 9.47 us: sum_over_rows(): lax.dot_general(left_side, right_side, (((0,), (0,)), ((), ())), preferre...]
    all_to_all x3 -> x0, starting transfers between devices: 20.3 us -> none  [the longest x1 12 us: sent_and_summed(): lax.all_to_all(tiles, axis, split_axis=0, concat_axis=0, tiled=True)]
    all_to_all x3 -> x0, waiting for transfers between devices: 8.04 us -> none  [the longest x1 4.44 us: body(): lax.all_to_all(grad_up, DEPTH, split_axis=1, concat_axis=0, tiled=True)]
  transfers between devices with their start and end apart: 5 -> 0, of which waited for: 3 -> 0; matrix products, arithmetic and copies ran while one was open for 10% -> 0% of each run, Pallas kernels for 0% -> 0%
where the time goes in v1:
time: 94.1 us; the launch traced here: 92.7 us
  Pallas kernels  85.3 us (91%)
  local copies, waits for them, and re-layouts  6.73 us (7%)
    pallas_call x1, Pallas kernels, body(): pl.pallas_call(kernel, out_shape=(jax.ShapeDtypeStruct(tokens.shape, BF16...  85.3 us
    unnamed x8, local copies, waits for them, and re-layouts  5.54 us

profile of v1, /device:TPU:1, one launch (start us, length us, event | category | flops | bytes accessed | tf_op | source)
XLA Modules:
  0.0 92.7 jit_solution(18269198232242693435)
XLA Ops:
  0.6 85.3 %shard_map.92 = (bf16[8,1152]{1,0:T(8,128)(2,1)}, f32[144,1152]{1,0:T(8,128)}, f32[144,1152]{1,0:T(8,128)}, f32[144,1152]{1,0:T(8,128)}, f32[8,128]{1,0:T(8,128)}) custom-call(bf16[8,1152]{1,0:T(8,128)(2,1)} %x_ref.1, bf16[8,1152]{1,0:T(8,128)(2,1)} %dy_ref.1, bf16[144,1152]{1,0:T(8,128)(2,1)} %wg_ref.1, bf16[144,1152]{1,0:T(8,128)(2,1)} %wu_ref.1, ...), custom_call_target="tpu_custom_call" | custom-call | tf_op jit(solution)/shard_map/pallas_call | solution.py:384
  85.9 1.2 %slice_bitcast_fusion = f32[3]{0:T(128)} fusion(f32[8,128]{1,0:T(8,128)} %get-tuple-element.14), kind=kLoop, calls=%fused_computation | loop fusion | bytes 24 | tf_op jit(solution)/shard_map/squeeze | solution.py:426
  87.1 1.3 %copy.14 = bf16[8,1152]{1,0:T(8,128)(2,1)} copy(bf16[8,1152]{1,0:T(8,128)(2,1)} %get-tuple-element.20) | data formatting | bytes 36864
  88.5 0.0 copy-start.1
  88.5 2.0 %copy.15 = f32[144,1152]{1,0:T(8,128)} copy(f32[144,1152]{1,0:T(8,128)} %get-tuple-element.21) | data formatting | bytes 1327104
  90.5 0.0 copy-done.1
  90.5 0.0 copy-start
  90.5 0.8 copy.16
  91.4 0.5 copy-done
  91.8 0.8 copy.17
Async XLA Ops:
  88.5 2.0 %copy-start.1 = (f32[144,1152]{1,0:T(8,128)S(1)}, f32[144,1152]{1,0:T(8,128)}, u32[]{:S(2)}) copy-start(f32[144,1152]{1,0:T(8,128)} %get-tuple-element.22) | copy-start | bytes 1990660
  90.5 1.3 %copy-start = (f32[144,1152]{1,0:T(8,128)S(1)}, f32[144,1152]{1,0:T(8,128)}, u32[]{:S(2)}) copy-start(f32[144,1152]{1,0:T(8,128)} %get-tuple-element.23) | copy-start | bytes 1990660

commit v2 on v1

v2 whole, which is shorter than its diff:
```python
import functools

import jax
import jax.numpy as jnp
from jax import lax
from jax.experimental import pallas as pl
from jax.experimental.pallas import tpu as pltpu
from jax.sharding import Mesh
from jax.sharding import PartitionSpec as P

D = 4608
FF = 18432
ROW_DEPTH = ("row", "depth_0", "depth_1")
Z, X, Y = 16, 4, 4
STEPS = Z // 2
F32 = jnp.float32
BF16 = jnp.bfloat16
MESH = pl.DeviceIdType.MESH

tanh_scale = 0.7978845608028654
cubic_coeff = 0.044715


def gelu_parts(pre_act):
    inner_arg = tanh_scale * (pre_act + cubic_coeff * pre_act * pre_act * pre_act)
    tanh_value = jnp.tanh(inner_arg)
    gelu_value = 0.5 * pre_act * (1.0 + tanh_value)
    gelu_slope = 0.5 * (1.0 + tanh_value) + 0.5 * pre_act * (
        1.0 - tanh_value * tanh_value
    ) * tanh_scale * (1.0 + 3.0 * cubic_coeff * pre_act * pre_act)
    return (gelu_value, gelu_slope)


def geglu_backward(gate_pre, up_pre, grad_hidden):
    gelu_value, gelu_slope = gelu_parts(gate_pre)
    return (
        gelu_value * up_pre,
        grad_hidden * up_pre * gelu_slope,
        grad_hidden * gelu_value,
    )


def nt(a, b):
    return lax.dot_general(a, b, (((1,), (1,)), ((), ())), preferred_element_type=F32)


def nn(a, b):
    return lax.dot_general(a, b, (((1,), (0,)), ((), ())), preferred_element_type=F32)


def tn(a, b):
    return lax.dot_general(a, b, (((0,), (0,)), ((), ())), preferred_element_type=F32)


def kernel(
    x_ref, dy_ref, wg_ref, wu_ref, wd_ref,
    gi_out, w_out, rms_out,
    blk, wm, wlx, wld, pf, sx, rx, g, xs, mxs, mg, gi, sy, ry, sz, rz, acc,
    plane, line, sb,
    ysend, yrecv, wlocal, wsend, wrecv, fsend, frecv,
    xsend, xrecv, gsend, grecv, rysend, ryrecv, rzsend, rzrecv,
    mxsend, mxrecv, mgsend, mgrecv, nsend, nrecv,
):
    z = lax.axis_index("row")
    x = lax.axis_index("col")
    y = lax.axis_index("depth_0")
    k = lax.axis_index("depth_1")

    def zdev(o):
        return {"row": lax.rem(z + o, Z)}

    def xdev(o):
        return {"col": lax.rem(x + o, X)}

    def ydev(o):
        return {"depth_0": lax.rem(y + o, Y)}

    mate = {"depth_1": 1 - k}

    def rcopy(src, dst, s, r, dev):
        return pltpu.make_async_remote_copy(
            src_ref=src, dst_ref=dst, send_sem=s, recv_sem=r, device_id=dev, device_id_type=MESH
        )

    def wait_bytes(ref, sem, name="w"):
        with jax.named_scope("wait_" + name):
            pltpu.make_async_copy(ref, ref, sem).wait()

    barrier = pltpu.get_barrier_semaphore()
    near = [zdev(1), zdev(Z - 1), mate]
    near += [xdev(o) for o in range(1, X)] + [ydev(o) for o in range(1, Y)]
    for dev in near:
        pl.semaphore_signal(barrier, inc=1, device_id=dev, device_id_type=MESH)

    weights = (wg_ref, wu_ref, wd_ref)

    def tail_of(p):
        return (wlx, 0) if p == 0 else (wlx, 32) if p == 1 else (wld, 64)

    local = []
    for p in range(3):
        tail, at = tail_of(p)
        local.append(
            pltpu.make_async_copy(weights[p].at[0:128], wm.at[p, 0:128], wlocal.at[2 * p])
        )
        local.append(
            pltpu.make_async_copy(
                weights[p].at[128:144], tail.at[at : at + 16], wlocal.at[2 * p + 1]
            )
        )
    for c in local:
        c.start()
    wlx[64:128, :] = jnp.zeros((64, wlx.shape[1]), BF16)
    wld[0:64, :] = jnp.zeros((64, wld.shape[1]), BF16)
    wld[96:128, :] = jnp.zeros((32, wld.shape[1]), BF16)
    blk[0, 0, 0, pl.ds(y, 1)] = x_ref[...][None]
    blk[0, 0, 1, pl.ds(y, 1)] = dy_ref[...][None]

    with jax.named_scope("barrier"):
        pl.semaphore_wait(barrier, len(near))

    ycopies = []
    for xd, src in ((0, x_ref), (1, dy_ref)):
        for o in (2, 1, 3):
            c = rcopy(
                src, blk.at[0, 0, xd, y], ysend.at[xd, o - 1], yrecv.at[xd, o - 1], ydev(o)
            )
            c.start()
            ycopies.append(c)
    wcopies = []
    for p in range(3):
        tail, at = tail_of(p)
        wcopies.append(
            rcopy(
                weights[p].at[0:128], wm.at[p, 128:256], wsend.at[2 * p], wrecv.at[2 * p], mate
            )
        )
        wcopies.append(
            rcopy(
                weights[p].at[128:144],
                tail.at[at + 16 : at + 32],
                wsend.at[2 * p + 1],
                wrecv.at[2 * p + 1],
                mate,
            )
        )
    for c in wcopies:
        c.start()

    def quarter(direction, slot, q):
        half = 2 * (q % 2)
        return blk.at[direction, slot, q // 2, half : half + 2]

    def ring(direction, src_dir, src_slot, dst_dir, dst_slot, q):
        return rcopy(
            quarter(src_dir, src_slot, q),
            quarter(dst_dir, dst_slot, q),
            fsend.at[direction, src_slot, q],
            frecv.at[dst_dir, dst_slot, q],
            zdev(1) if direction == 0 else zdev(Z - 1),
        )

    for xd in range(2):
        with jax.named_scope("wait_y"):
            for o in range(3):
                ycopies[3 * xd + o].wait_recv()
        for q in (2 * xd, 2 * xd + 1):
            ring(0, 0, 0, 0, 1, q).start()
            ring(1, 0, 0, 1, 1, q).start()

    with jax.named_scope("wait_w"):
        for c in local:
            c.wait()
        for c in wcopies:
            c.wait_recv()

    def got(direction, slot, q):
        wait_bytes(quarter(direction, slot, q), frecv.at[direction, slot, q], "ring")

    def poll(t, q):
        @pl.when(t < STEPS)
        def _():
            for direction in range(2):
                got(direction, t, q)

                @pl.when(t < STEPS - 1)
                def _():
                    ring(direction, direction, t, direction, t + 1, q).start()

                if direction == q // 2:

                    @pl.when(t == STEPS - 1)
                    def _():
                        ring(direction, direction, t, 1, 0, q).start()

        @pl.when(t == STEPS)
        def _():
            got(1, 0, q)

    def rows_of(t, xd):
        slot = lax.rem(t, STEPS)
        return blk[:, pl.ds(slot, 1), xd].astype(F32).reshape(64, -1).astype(BF16)

    def put(i, value, at):
        pf[pl.ds(i, 1), :, :, at : at + value.shape[1]] = value.reshape(1, X, 16, -1)

    def to_mate(src, dst, s, r):
        rcopy(src, dst, s, r, mate).start()

    lane = lax.broadcasted_iota(jnp.int32, (16, 128), 1)

    def stage_b(i):
        wait_bytes(rx.at[i], xrecv.at[i], "rx")
        total = pf[i, x]
        for o in range(3):
            total = total + rx[i, o].astype(F32)
        hid, gg, gu = geglu_backward(total[:, 0:256], total[:, 256:512], total[:, 512:768])
        left = total[:, 768:896]
        hid_l, gg_l, gu_l = geglu_backward(
            left, pltpu.roll(left, 96, 1), pltpu.roll(left, 64, 1)
        )
        packed = jnp.where(
            lane < 32,
            gg_l,
            jnp.where(
                lane < 64,
                pltpu.roll(gu_l, 32, 1),
                jnp.where(lane < 96, pltpu.roll(hid_l, 64, 1), 0.0),
            ),
        )
        g[i, x, :, 0:256] = gg.astype(BF16)
        g[i, x, :, 256:512] = gu.astype(BF16)
        g[i, x, :, 512:768] = hid.astype(BF16)
        g[i, x, :, 768:896] = packed.astype(BF16)
        for o in (2, 1, 3):
            rcopy(g.at[i, x], g.at[i, x], gsend.at[i], grecv.at[i], xdev(o)).start()

    def stage_c(i):
        wait_bytes(g.at[i, 0:3], grecv.at[i], "g")
        to_mate(g.at[i], mg.at[i], mgsend.at[i], mgrecv.at[i])
        gv = g[i].reshape(64, 896)
        part = (
            nn(gv[:, 0:256], wm[0]) + nn(gv[:, 256:512], wm[1]) + nn(gv[:, 768:896], wlx[...])
        )
        gi[pl.ds(i, 1)] = part.reshape(1, 2, Y, 8, -1)
        for o in (2, 1, 3):
            j = lax.rem(y + o, Y)
            sy[i, o - 1] = gi[i, :, j].astype(BF16)
            rcopy(
                sy.at[i, o - 1], ry.at[i, o - 1], rysend.at[i], ryrecv.at[i], ydev(o)
            ).start()

    def stage_d(i):
        wait_bytes(ry.at[i], ryrecv.at[i], "ry")
        total = gi[i, :, y]
        for o in range(3):
            total = total + ry[i, o].astype(F32)
        sz[i] = total.astype(BF16)
        t = i + 1

        @pl.when(t < STEPS)
        def _():
            rcopy(
                sz.at[i, 0], rz.at[t - 1], rzsend.at[i, 0], rzrecv, zdev(Z - t)
            ).start()

        @pl.when(t == STEPS)
        def _():
            acc[...] = total[0]

        rcopy(
            sz.at[i, 1], rz.at[STEPS - 2 + t], rzsend.at[i, 1], rzrecv, zdev(t)
        ).start()

    def scoped(f, name):
        def inner(*args):
            with jax.named_scope("stage_" + name):
                f(*args)
        return inner

    stage_b, stage_c, stage_d = scoped(stage_b, "b"), scoped(stage_c, "c"), scoped(stage_d, "d")

    def step(t, carry):
        i = t - 1
        poll(t, 0)
        poll(t, 1)
        pl.when(t >= 3)(lambda: stage_b(t - 3))
        with jax.named_scope("a_x"):
            xv = rows_of(t, 0)
            xs[0, pl.ds(i, 1)] = xv[None]
            put(i, nt(xv, wm[0]), 0)
            put(i, nt(xv, wm[1]), 256)
            left = nt(xv, wlx[...])
        poll(t, 2)
        pl.when(t >= 5)(lambda: stage_c(t - 5))
        poll(t, 3)
        with jax.named_scope("a_d"):
            dv = rows_of(t, 1)
            xs[1, pl.ds(i, 1)] = dv[None]
            put(i, nt(dv, wm[2]), 512)
            put(i, left + nt(dv, wld[...]), 768)
            for o in (2, 1, 3):
                j = lax.rem(x + o, X)
                sx[i, o - 1] = pf[i, j].astype(BF16)
                rcopy(
                    sx.at[i, o - 1], rx.at[i, o - 1], xsend.at[i], xrecv.at[i], xdev(o)
                ).start()
            for xd in range(2):
                to_mate(xs.at[xd, i], mxs.at[xd, i], mxsend.at[xd, i], mxrecv.at[xd, i])
        pl.when(t >= 7)(lambda: stage_d(t - 7))
        return carry

    lax.fori_loop(1, STEPS + 1, step, 0)

    def own(lanes, first, last, source):
        count = 64 * (last - first)
        return source[first:last].reshape(count, 896)[:, lanes : lanes + 128]

    def wgrad_of(first, last, gsrc, xsrc):
        count = 64 * (last - first)
        xa = xsrc[0, first:last].reshape(count, -1)
        da = xsrc[1, first:last].reshape(count, -1)
        tail = own(768, first, last, gsrc)
        tail_x, tail_d = tn(tail, xa), tn(tail, da)
        return (
            (tn(own(0, first, last, gsrc), xa), tail_x, 0),
            (tn(own(256, first, last, gsrc), xa), tail_x, 32),
            (tn(own(512, first, last, gsrc), da), tail_d, 64),
        )

    def wgrad_mine(first, last, fresh):
        for p, (main, tail, at) in enumerate(wgrad_of(first, last, g, xs)):
            low = tail[at : at + 16]
            w_out[p, 0:128] = main if fresh else w_out[p, 0:128] + main
            w_out[p, 128:144] = low if fresh else w_out[p, 128:144] + low

    def mate_own(lanes, first, last):
        return own(lanes + 128, first, last, mg)

    def wgrad_mate(first, last):
        for i in range(first, last):
            wait_bytes(mg.at[i], mgrecv.at[i], "mg")
            for xd in range(2):
                wait_bytes(mxs.at[xd, i], mxrecv.at[xd, i], "mx")
        count = 64 * (last - first)
        xa = mxs[0, first:last].reshape(count, -1)
        da = mxs[1, first:last].reshape(count, -1)
        tail = own(768, first, last, mg)
        tail_x, tail_d = tn(tail, xa), tn(tail, da)
        for p, (right, tails, at) in enumerate(
            ((xa, tail_x, 16), (xa, tail_x, 48), (da, tail_d, 80))
        ):
            w_out[p, 0:128] = w_out[p, 0:128] + tn(mate_own(256 * p, first, last), right)
            w_out[p, 128:144] = w_out[p, 128:144] + tails[at : at + 16]

    half = STEPS // 2
    stage_b(STEPS - 2)
    stage_c(STEPS - 4)
    stage_d(STEPS - 6)
    with jax.named_scope("wgrad_1"):
        wgrad_mine(0, half, True)
        wgrad_mate(0, half)
    stage_b(STEPS - 1)
    stage_c(STEPS - 3)
    stage_d(STEPS - 5)
    stage_c(STEPS - 2)
    stage_d(STEPS - 4)
    with jax.named_scope("wgrad_2"):
        wgrad_mine(half, STEPS - 1, False)
        wgrad_mate(half, STEPS - 1)
    stage_c(STEPS - 1)
    stage_d(STEPS - 3)
    stage_d(STEPS - 2)
    with jax.named_scope("wgrad_3"):
        wgrad_mine(STEPS - 1, STEPS, False)
        wgrad_mate(STEPS - 1, STEPS)

    with jax.named_scope("squares"):
        lanes = lax.broadcasted_iota(jnp.int32, (8, 128), 1)
        value = jnp.zeros((8, 128), F32)
        for p in range(3):
            total = w_out[p]
            square = jnp.sum((total * total).reshape(18, 8, -1), axis=0)
            value = jnp.where(lanes == p, jnp.sum(square), value)

    here = (x * Y + y) * 2 + k
    sb[0] = value
    plane[here] = value
    for dx in (2, 1, 3, 0):
        for dy in (2, 1, 3, 0):
            for dk in (1, 0):
                if dx or dy or dk:
                    rcopy(
                        sb.at[0],
                        plane.at[here],
                        nsend.at[0],
                        nrecv.at[0],
                        {
                            "col": lax.rem(x + dx, X),
                            "depth_0": lax.rem(y + dy, Y),
                            "depth_1": lax.rem(k + dk, 2),
                        },
                    ).start()
    stage_d(STEPS - 1)
    others = X * Y * 2 - 1
    wait_bytes(plane.at[0:others], nrecv.at[0], "plane")
    value = jnp.sum(plane[...], axis=0)
    sb[1] = value
    line[z] = value
    for o in range(Z // 2, 0, -1):
        for d in sorted({o, Z - o}):
            rcopy(sb.at[1], line.at[z], nsend.at[1], nrecv.at[1], zdev(d)).start()

    wait_bytes(rz, rzrecv, "rz")
    total = acc[...]
    for j in range(Z - 1):
        total = total + rz[j].astype(F32)
    gi_out[...] = total.astype(BF16)

    for c in ycopies:
        c.wait_send()
    for c in wcopies:
        c.wait_send()
    for s in range(STEPS):
        for q in range(4):
            for direction in range(2):
                if s < STEPS - 1 or direction == q // 2:
                    wait_bytes(quarter(direction, 0, q), fsend.at[direction, s, q])
        wait_bytes(sx.at[s], xsend.at[s])
        wait_bytes(g.at[s, 0:3], gsend.at[s])
        wait_bytes(mg.at[s], mgsend.at[s])
        for xd in range(2):
            wait_bytes(mxs.at[xd, s], mxsend.at[xd, s])
        wait_bytes(sy.at[s], rysend.at[s])
        if s < STEPS - 1:
            wait_bytes(sz.at[s, 0], rzsend.at[s, 0])
        wait_bytes(sz.at[s, 1], rzsend.at[s, 1])
    wait_bytes(plane.at[0:others], nsend.at[0])

    wait_bytes(line.at[0 : Z - 1], nrecv.at[1], "line")
    rms_out[...] = jnp.sqrt(jnp.sum(line[...], axis=0) / F32(D * FF))
    wait_bytes(line.at[0 : Z - 1], nsend.at[1])


def finish(gi_ref, w_ref, rms_ref, gi_out, gw_out, uw_out, dw_out, rms_out, sems):
    copies = [
        pltpu.make_async_copy(w_ref.at[p], out, sems.at[p])
        for p, out in enumerate((gw_out, uw_out, dw_out))
    ]
    copies.append(pltpu.make_async_copy(gi_ref, gi_out, sems.at[3]))
    for c in copies:
        c.start()
    row = rms_ref[0:1, :]
    lanes = lax.broadcasted_iota(jnp.int32, row.shape, 1)
    for p in range(3):
        rms_out[p] = jnp.sum(jnp.where(lanes == p, row, 0.0))
    for c in copies:
        c.wait()


def body(tokens, grad_out, w_gate, w_up, w_down):
    c = tokens.shape[1]
    h = w_gate.shape[0]
    vmem = pl.BlockSpec(memory_space=pltpu.VMEM)
    hbm = pl.BlockSpec(memory_space=pl.ANY)
    dma = pltpu.SemaphoreType.DMA
    grad_in, wgrads, rms = pl.pallas_call(
        kernel,
        out_shape=(
            pltpu.VMEM(tokens.shape, BF16),
            pltpu.VMEM((3, h, c), F32),
            pltpu.VMEM((8, 128), F32),
        ),
        in_specs=[vmem, vmem, hbm, hbm, hbm],
        out_specs=(vmem, vmem, vmem),
        scratch_shapes=[
            pltpu.VMEM((2, STEPS, 2, Y, 8, c), BF16),
            pltpu.VMEM((3, 256, c), BF16),
            pltpu.VMEM((128, c), BF16),
            pltpu.VMEM((128, c), BF16),
            pltpu.VMEM((STEPS, X, 16, 896), F32),
            pltpu.VMEM((STEPS, 3, 16, 896), BF16),
            pltpu.VMEM((STEPS, 3, 16, 896), BF16),
            pltpu.VMEM((STEPS, X, 16, 896), BF16),
            pltpu.VMEM((2, STEPS, 64, c), BF16),
            pltpu.VMEM((2, STEPS, 64, c), BF16),
            pltpu.VMEM((STEPS, X, 16, 896), BF16),
            pltpu.VMEM((STEPS, 2, Y, 8, c), F32),
            pltpu.VMEM((STEPS, 3, 2, 8, c), BF16),
            pltpu.VMEM((STEPS, 3, 2, 8, c), BF16),
            pltpu.VMEM((STEPS, 2, 8, c), BF16),
            pltpu.VMEM((Z - 1, 8, c), BF16),
            pltpu.VMEM((8, c), F32),
            pltpu.VMEM((X * Y * 2, 8, 128), F32),
            pltpu.VMEM((Z, 8, 128), F32),
            pltpu.VMEM((2, 8, 128), F32),
            dma((2, 3)), dma((2, 3)), dma((6,)), dma((6,)), dma((6,)),
            dma((2, STEPS, 4)), dma((2, STEPS, 4)),
            dma((STEPS,)), dma((STEPS,)), dma((STEPS,)), dma((STEPS,)),
            dma((STEPS,)), dma((STEPS,)), dma((STEPS, 2)), dma,
            dma((2, STEPS)), dma((2, STEPS)), dma((STEPS,)), dma((STEPS,)),
            dma((2,)), dma((2,)),
        ],
        compiler_params=pltpu.CompilerParams(
            collective_id=0, has_side_effects=True, vmem_limit_bytes=64_700_000
        ),
    )(tokens, grad_out, w_gate, w_up, w_down)
    wgrad = jax.ShapeDtypeStruct((h, c), F32)
    return pl.pallas_call(
        finish,
        out_shape=(
            jax.ShapeDtypeStruct(tokens.shape, BF16),
            wgrad,
            wgrad,
            wgrad,
            jax.ShapeDtypeStruct((3,), F32),
        ),
        in_specs=[hbm, hbm, vmem],
        out_specs=(hbm, hbm, hbm, hbm, pl.BlockSpec(memory_space=pltpu.SMEM)),
        scratch_shapes=[dma((4,))],
        compiler_params=pltpu.CompilerParams(vmem_limit_bytes=1024 * 1024),
    )(grad_in, wgrads, rms)


def solution(mesh):
    torus = Mesh(
        mesh.devices.reshape(mesh.shape["row"], mesh.shape["col"], 4, 2),
        ("row", "col", "depth_0", "depth_1"),
    )
    placed = P(ROW_DEPTH, "col")
    return jax.shard_map(
        body,
        mesh=torus,
        in_specs=(placed,) * 5,
        out_specs=(placed, placed, placed, placed, P()),
        check_vma=False,
    )
```

time: 94.1 us -> 77.3 us (0.82); the launches traced: 92.7 us -> 77.1 us
  Pallas kernels: 85.3 us -> 76.5 us
  local copies, waits for them, and re-layouts: 6.73 us -> 0 us
    pallas_call x1 -> x2, Pallas kernels: 85.3 us -> 76.5 us  [the longest x1 74.6 us: body(): pl.pallas_call(kernel, out_shape=(pltpu.VMEM(tokens.shape, BF16), pltpu.V...]
    unnamed x8 -> x0, local copies, waits for them, and re-layouts: 5.54 us -> none
    squeeze x1 -> x0, local copies, waits for them, and re-layouts: 1.2 us -> none  [body(): return (grad_in, gw, uw, dw, rms[0, 0:3])]
where the time goes in v2:
time: 77.3 us; the launch traced here: 77.1 us
  Pallas kernels  76.5 us (99%)
    pallas_call x1, Pallas kernels, body(): pl.pallas_call(kernel, out_shape=(pltpu.VMEM(tokens.shape, BF16), pltpu.V...  74.6 us
    pallas_call x1, Pallas kernels, body(): pl.pallas_call(finish, out_shape=(jax.ShapeDtypeStruct(tokens.shape, BF16...  1.83 us

profile of v2, /device:TPU:1, one launch (start us, length us, event | category | flops | bytes accessed | tf_op | source)
XLA Modules:
  0.0 77.1 jit_solution(9567285873049778869)
XLA Ops:
  0.6 74.6 %shard_map.92 = (bf16[8,1152]{1,0:T(8,128)(2,1)S(1)}, f32[3,144,1152]{2,1,0:T(8,128)S(1)}, f32[8,128]{1,0:T(8,128)S(1)}) custom-call(bf16[8,1152]{1,0:T(8,128)(2,1)} %x_ref.1, bf16[8,1152]{1,0:T(8,128)(2,1)} %dy_ref.1, bf16[144,1152]{1,0:T(8,128)(2,1)} %wg_ref.1, bf16[144,1152]{1,0:T(8,128)(2,1)} %wu_ref.1, bf16[144,1152]{1,0:T(8,128)(2,1)} %wd_ref.1), custom_call_target="tpu_custom_call" | custom-call | tf_op jit(solution)/shard_map/pallas_call | solution.py:467
  75.3 1.8 %shard_map.93 = (bf16[8,1152]{1,0:T(8,128)(2,1)}, f32[144,1152]{1,0:T(8,128)}, f32[144,1152]{1,0:T(8,128)}, f32[144,1152]{1,0:T(8,128)}, f32[3]{0:T(128)}) custom-call(bf16[8,1152]{1,0:T(8,128)(2,1)S(1)} %get-tuple-element.8.gi_ref, f32[3,144,1152]{2,1,0:T(8,128)S(1)} %get-tuple-element.9.w_ref, f32[8,128]{1,0:T(8,128)S(1)} %get-tuple-element.10.rms_ref), custom_call_target="tpu_custom_call" | custom-call | tf_op jit(solution)/shard_map/pallas_call | solution.py:509

commit v3 on v2

v3 whole, which is shorter than its diff:
```python
import functools

import jax
import jax.numpy as jnp
from jax import lax
from jax.experimental import pallas as pl
from jax.experimental.pallas import tpu as pltpu
from jax.sharding import Mesh
from jax.sharding import PartitionSpec as P

D = 4608
FF = 18432
ROW_DEPTH = ("row", "depth_0", "depth_1")
Z, X, Y = 16, 4, 4
STEPS = Z // 2
ZL = 384
CHUNKS = 4
F32 = jnp.float32
BF16 = jnp.bfloat16
MESH = pl.DeviceIdType.MESH

tanh_scale = 0.7978845608028654
cubic_coeff = 0.044715


def gelu_parts(pre_act):
    inner_arg = tanh_scale * (pre_act + cubic_coeff * pre_act * pre_act * pre_act)
    tanh_value = jnp.tanh(inner_arg)
    gelu_value = 0.5 * pre_act * (1.0 + tanh_value)
    gelu_slope = 0.5 * (1.0 + tanh_value) + 0.5 * pre_act * (
        1.0 - tanh_value * tanh_value
    ) * tanh_scale * (1.0 + 3.0 * cubic_coeff * pre_act * pre_act)
    return (gelu_value, gelu_slope)


def geglu_backward(gate_pre, up_pre, grad_hidden):
    gelu_value, gelu_slope = gelu_parts(gate_pre)
    return (
        gelu_value * up_pre,
        grad_hidden * up_pre * gelu_slope,
        grad_hidden * gelu_value,
    )


def nt(a, b):
    return lax.dot_general(a, b, (((1,), (1,)), ((), ())), preferred_element_type=F32)


def nn(a, b):
    return lax.dot_general(a, b, (((1,), (0,)), ((), ())), preferred_element_type=F32)


def tn(a, b):
    return lax.dot_general(a, b, (((0,), (0,)), ((), ())), preferred_element_type=F32)


def kernel(
    x_ref, dy_ref, wg_ref, wu_ref, wd_ref,
    gi_out, w_out, rms_out,
    blk, wm, wlx, wld, pf, sx, rx, g, xs, ga, gb, gi, sy, ry, sz, rz, acc,
    plane, line, sb, wacc,
    feed, ysend, yrecv, wlocal, wsend, wrecv, send, frecv, urecv, vrecv,
    xgsend, xrecv, grecv, ryrecv, rzsend, rzrecv,
    mxrecv, mgsend, mgrecv, nsend, nrecv, wsem,
):
    z = lax.axis_index("row")
    x = lax.axis_index("col")
    y = lax.axis_index("depth_0")
    k = lax.axis_index("depth_1")

    def zdev(o):
        return {"row": lax.rem(z + o, Z)}

    def xdev(o):
        return {"col": lax.rem(x + o, X)}

    def ydev(o):
        return {"depth_0": lax.rem(y + o, Y)}

    mate = {"depth_1": 1 - k}

    def rcopy(src, dst, s, r, dev):
        return pltpu.make_async_remote_copy(
            src_ref=src, dst_ref=dst, send_sem=s, recv_sem=r, device_id=dev, device_id_type=MESH
        )

    def wait_bytes(ref, sem, name="w"):
        with jax.named_scope("wait_" + name):
            pltpu.make_async_copy(ref, ref, sem).wait()

    barrier = pltpu.get_barrier_semaphore()
    near = [zdev(1), zdev(Z - 1), mate]
    near += [xdev(o) for o in range(1, X)] + [ydev(o) for o in range(1, Y)]
    for dev in near:
        pl.semaphore_signal(barrier, inc=1, device_id=dev, device_id_type=MESH)

    weights = (wg_ref, wu_ref, wd_ref)

    def tail_of(p):
        return (wlx, 0) if p == 0 else (wlx, 32) if p == 1 else (wld, 64)

    local = []
    for p in range(3):
        tail, at = tail_of(p)
        local.append(
            pltpu.make_async_copy(weights[p].at[0:128], wm.at[p, 0:128], wlocal.at[p])
        )
        local.append(
            pltpu.make_async_copy(
                weights[p].at[128:144], tail.at[at : at + 16], wlocal.at[p]
            )
        )
    feeds = [
        pltpu.make_async_copy(src, blk.at[0, 0, xd, y], feed)
        for xd, src in ((0, x_ref), (1, dy_ref))
    ]
    for c in feeds + local:
        c.start()
    wlx[64:128, :] = jnp.zeros((64, wlx.shape[1]), BF16)
    wld[0:64, :] = jnp.zeros((64, wld.shape[1]), BF16)
    wld[96:128, :] = jnp.zeros((32, wld.shape[1]), BF16)
    wait_bytes(blk.at[0, 0, 0, 0:2], feed)

    with jax.named_scope("barrier"):
        pl.semaphore_wait(barrier, len(near))

    def chunk(direction, slot, q):
        at = ZL * max(q - 1, 0)
        return blk.at[direction, slot, min(q, 1), :, :, at : at + ZL]

    def unit(direction, slot):
        return blk.at[direction, slot, 0, y, :, ZL:]

    def along(direction):
        return zdev(1) if direction == 0 else zdev(Z - 1)

    def ring(direction, src_dir, src_slot, dst_dir, dst_slot, q, t):
        return rcopy(
            chunk(src_dir, src_slot, q),
            chunk(dst_dir, dst_slot, q),
            send.at[src_slot],
            frecv.at[direction, lax.rem(t, 3), q],
            along(direction),
        )

    def unit_ring(direction, src_dir, src_slot, dst_dir, dst_slot, t):
        return rcopy(
            unit(src_dir, src_slot),
            unit(dst_dir, dst_slot),
            send.at[src_slot],
            urecv.at[direction, lax.rem(t, 3)],
            along(direction),
        )

    unit_ring(0, 0, 0, 0, 1, 1).start()
    unit_ring(1, 0, 0, 1, 1, 1).start()
    for o in (2, 1, 3):
        for xd in range(2):
            own_unit = blk.at[0, 0, xd, y]
            rcopy(own_unit, own_unit, ysend, yrecv.at[xd], ydev(o)).start()

    def enter(q):
        ring(0, 0, 0, 0, 1, q, 1).start()
        ring(1, 0, 0, 1, 1, q, 1).start()

    for p in range(3):
        tail, at = tail_of(p)
        rcopy(
            weights[p].at[0:128], wm.at[p, 128:256], wsend.at[p], wrecv.at[p], mate
        ).start()
        rcopy(
            weights[p].at[128:144], tail.at[at + 16 : at + 32], wsend.at[p], wrecv.at[p], mate
        ).start()

    wait_bytes(blk.at[0, 0, 0, 0:3], yrecv.at[0], "y")
    enter(0)
    wait_bytes(blk.at[0, 0, 1, 0:3], yrecv.at[1], "y")
    for q in range(1, CHUNKS):
        enter(q)

    for p in range(3):
        wait_bytes(wm.at[0, 0:144], wlocal.at[p], "w")
        wait_bytes(wm.at[0, 0:144], wrecv.at[p], "w")

    def got(direction, slot, q, t, way):
        wait_bytes(chunk(direction, slot, q), frecv.at[way, lax.rem(t, 3), q], "ring")

    def last_way(q):
        return 0 if q < 2 else 1

    def poll(t, q):
        @pl.when(t < STEPS)
        def _():
            for direction in range(2):
                got(direction, t, q, t, direction)

                @pl.when(t < STEPS - 1)
                def _():
                    ring(direction, direction, t, direction, t + 1, q, t + 1).start()

                if direction == last_way(q):

                    @pl.when(t == STEPS - 1)
                    def _():
                        ring(direction, direction, t, 1, 0, q, t + 1).start()

        @pl.when(t == STEPS)
        def _():
            got(1, 0, q, t, last_way(q))

    def spread(direction, slot, t):
        for o in (2, 1, 3):
            rcopy(
                unit(direction, slot),
                unit(direction, slot),
                send.at[t - 1],
                vrecv.at[lax.rem(t, 4)],
                ydev(o),
            ).start()

    def poll_unit(t):
        @pl.when(t < STEPS)
        def _():
            for direction in range(2):
                wait_bytes(unit(direction, t), urecv.at[direction, lax.rem(t, 3)], "unit")

                @pl.when(t < STEPS - 1)
                def _():
                    unit_ring(direction, direction, t, direction, t + 1, t + 1).start()

                if direction == 0:

                    @pl.when(t == STEPS - 1)
                    def _():
                        unit_ring(0, 0, t, 1, 0, t + 1).start()

                spread(direction, t, t)

        @pl.when(t == STEPS)
        def _():
            wait_bytes(unit(1, 0), urecv.at[0, lax.rem(t, 3)], "unit")
            spread(1, 0, t)

    def wait_spread(t):
        @pl.when(t < STEPS)
        def _():
            wait_bytes(blk.at[:, t, 0, 0:3, :, ZL:], vrecv.at[lax.rem(t, 4)], "spread")

        @pl.when(t == STEPS)
        def _():
            wait_bytes(blk.at[1, 0, 0, 0:3, :, ZL:], vrecv.at[lax.rem(t, 4)], "spread")

    poll_unit(1)

    def rows_of(t, xd):
        slot = lax.rem(t, STEPS)
        return blk[:, pl.ds(slot, 1), xd].astype(F32).reshape(64, -1).astype(BF16)

    def put(i, value, at):
        pf[pl.ds(i, 1), :, :, at : at + value.shape[1]] = value.reshape(1, X, 16, -1)

    def to_mate(src, dst, s, r):
        rcopy(src, dst, s, r, mate).start()

    lane = lax.broadcasted_iota(jnp.int32, (16, 128), 1)

    def stage_b(i):
        wait_bytes(rx.at[i], xrecv.at[i], "rx")
        total = pf[i, x]
        for o in range(3):
            total = total + rx[i, o].astype(F32)
        hid, gg, gu = geglu_backward(total[:, 0:256], total[:, 256:512], total[:, 512:768])
        left = total[:, 768:896]
        hid_l, gg_l, gu_l = geglu_backward(
            left, pltpu.roll(left, 96, 1), pltpu.roll(left, 64, 1)
        )
        packed = jnp.where(
            lane < 32,
            gg_l,
            jnp.where(
                lane < 64,
                pltpu.roll(gu_l, 32, 1),
                jnp.where(lane < 96, pltpu.roll(hid_l, 64, 1), 0.0),
            ),
        )
        g[i, x, :, 0:256] = gg.astype(BF16)
        g[i, x, :, 256:512] = gu.astype(BF16)
        g[i, x, :, 512:768] = hid.astype(BF16)
        g[i, x, :, 768:896] = packed.astype(BF16)
        for o in (2, 1, 3):
            rcopy(g.at[i, x], g.at[i, x], xgsend.at[i], grecv.at[i], xdev(o)).start()

    def stage_c(i):
        wait_bytes(g.at[i, 0:3], grecv.at[i], "g")
        gv = g[i].reshape(64, 896)
        tail = gv[:, 768:896]
        for p in range(3):
            gb[i, :, 128 * p : 128 * p + 128] = gv[:, 256 * p + 128 : 256 * p + 256]
        gb[i, :, 384:512] = pltpu.roll(tail.astype(F32), 112, 1).astype(BF16)
        to_mate(gb.at[i], ga.at[i, 1], mgsend, mgrecv.at[i])
        for p in range(3):
            ga[i, 0, :, 128 * p : 128 * p + 128] = gv[:, 256 * p : 256 * p + 128]
        ga[i, 0, :, 384:512] = tail
        part = (
            nn(gv[:, 0:256], wm[0]) + nn(gv[:, 256:512], wm[1]) + nn(gv[:, 768:896], wlx[...])
        )
        gi[pl.ds(i, 1)] = part.reshape(1, 2, Y, 8, -1)
        for o in (2, 1, 3):
            j = lax.rem(y + o, Y)
            sy[i, o - 1] = gi[i, :, j].astype(BF16)
            rcopy(
                sy.at[i, o - 1], ry.at[i, o - 1], send.at[i], ryrecv.at[i], ydev(o)
            ).start()

    def stage_d(i, last=False):
        wait_bytes(ry.at[i], ryrecv.at[i], "ry")
        total = gi[i, :, y]
        for o in range(3):
            total = total + ry[i, o].astype(F32)
        sz[i] = total.astype(BF16)
        t = i + 1

        @pl.when(t < STEPS)
        def _():
            rcopy(
                sz.at[i, 0], rz.at[t - 1], send.at[i], rzrecv, zdev(Z - t)
            ).start()

        @pl.when(t == STEPS)
        def _():
            acc[...] = total[0]

        rcopy(
            sz.at[i, 1],
            rz.at[STEPS - 2 + t],
            rzsend if last else send.at[i],
            rzrecv,
            zdev(t),
        ).start()

    def scoped(f, name):
        def inner(*args):
            with jax.named_scope("stage_" + name):
                f(*args)
        return inner

    stage_b, stage_c, stage_d = scoped(stage_b, "b"), scoped(stage_c, "c"), scoped(stage_d, "d")

    def wgrad(first, n, fresh, p):
        with jax.named_scope("wgrad"):
            if p == 0:
                for j in range(n):
                    wait_bytes(ga.at[first + j, 1], mgrecv.at[first + j], "mg")
                    wait_bytes(xs.at[:, first + j, 1], mxrecv.at[first + j], "mx")
            gv = ga[pl.ds(first, n)].reshape(128 * n, 512)
            right = xs[p // 2, pl.ds(first, n)].reshape(128 * n, -1)
            news = [(p, 0, tn(gv[:, 128 * p : 128 * p + 128], right))]
            if p != 1:
                tail = tn(gv[:, 384:512], right)
                if p == 0:
                    news += [(0, 128, tail[0:16]), (1, 128, tail[32:48])]
                else:
                    news += [(2, 128, tail[64:80])]
            squares = {}
            for q, at, new in news:
                rows = new.shape[0]
                if not fresh:
                    new = wacc[q, at : at + rows] + new
                wacc[q, at : at + rows] = new
                squares[q, at] = jnp.sum((new * new).reshape(rows // 8, 8, -1), axis=0)
            return squares

    def step(t, carry):
        i = t - 1
        poll(t, 0)
        poll(t, 1)
        pl.when(t < STEPS)(lambda: poll_unit(t + 1))
        poll(t, 2)
        pl.when(t >= 3)(lambda: stage_b(t - 3))
        with jax.named_scope("a_x"):
            wait_spread(t)
            xv = rows_of(t, 0)
            xs[0, pl.ds(i, 1), 0] = xv[None]
            put(i, nt(xv, wm[0]), 0)
            put(i, nt(xv, wm[1]), 256)
            left = nt(xv, wlx[...])
        poll(t, 3)
        pl.when(t >= 5)(lambda: stage_c(t - 5))
        with jax.named_scope("a_d"):
            dv = rows_of(t, 1)
            xs[1, pl.ds(i, 1), 0] = dv[None]
            put(i, nt(dv, wm[2]), 512)
            put(i, left + nt(dv, wld[...]), 768)
            for o in (2, 1, 3):
                j = lax.rem(x + o, X)
                sx[i, o - 1] = pf[i, j].astype(BF16)
                rcopy(
                    sx.at[i, o - 1], rx.at[i, o - 1], xgsend.at[i], xrecv.at[i], xdev(o)
                ).start()
            for xd in range(2):
                to_mate(
                    xs.at[xd, i, 0], xs.at[xd, i, 1], send.at[i], mxrecv.at[i]
                )
        pl.when(t >= 7)(lambda: stage_d(t - 7))
        return carry

    lax.fori_loop(1, STEPS + 1, step, 0)

    def more(first, n, fresh=False):
        for p in range(3):
            wgrad(first, n, fresh, p)

    stage_c(4)
    stage_d(2)
    stage_b(6)
    stage_c(5)
    stage_b(7)
    more(0, 4, True)
    stage_d(3)
    stage_c(6)
    stage_d(4)
    more(4, 2)
    stage_d(5)
    stage_c(7)
    squares = {}
    for p in range(3):
        squares.update(wgrad(6, 2, False, p))
    value = jnp.zeros((8, 128), F32)
    for p in range(3):
        value = jnp.where(lane[0:8] == p, jnp.sum(squares[p, 0] + squares[p, 128]), value)

    here = (x * Y + y) * 2 + k
    sb[0] = value
    plane[here] = value
    for dx in (2, 1, 3, 0):
        for dy in (2, 1, 3, 0):
            for dk in (1, 0):
                if dx or dy or dk:
                    rcopy(
                        sb.at[0],
                        plane.at[here],
                        nsend.at[0],
                        nrecv.at[0],
                        {
                            "col": lax.rem(x + dx, X),
                            "depth_0": lax.rem(y + dy, Y),
                            "depth_1": lax.rem(k + dk, 2),
                        },
                    ).start()
    wcopy = pltpu.make_async_copy(wacc, w_out, wsem)
    wcopy.start()
    stage_d(6)
    stage_d(7, True)
    others = X * Y * 2 - 1
    wait_bytes(plane.at[0:others], nrecv.at[0], "plane")
    value = jnp.sum(plane[...], axis=0)
    sb[1] = value
    line[z] = value
    for o in range(Z // 2, 0, -1):
        for d in sorted({o, Z - o}):
            rcopy(sb.at[1], line.at[z], nsend.at[1], nrecv.at[1], zdev(d)).start()

    wait_bytes(rz, rzrecv, "rz")
    total = acc[...]
    for j in range(Z - 1):
        total = total + rz[j].astype(F32)
    gi_out[...] = total.astype(BF16)

    wait_bytes(wacc.at[0, 0:24], ysend)
    for p in range(3):
        wait_bytes(wm.at[0, 0:144], wsend.at[p])
    for i in range(STEPS):
        wait_bytes(wacc.at[0:2, 0:80] if i < STEPS - 1 else wacc.at[0, 0:120], send.at[i])
        wait_bytes(pf.at[0, 0:3], xgsend.at[i])
    wait_bytes(ga.at[:, 0], mgsend)
    wait_bytes(sz.at[0, 1], rzsend)
    wait_bytes(plane.at[0:others], nsend.at[0])
    wcopy.wait()

    wait_bytes(line.at[0 : Z - 1], nrecv.at[1], "line")
    rms_out[...] = jnp.sqrt(jnp.sum(line[...], axis=0) / F32(D * FF))
    wait_bytes(line.at[0 : Z - 1], nsend.at[1])


def finish(gi_ref, w_ref, rms_ref, gi_out, gw_out, uw_out, dw_out, rms_out, sems):
    copies = [
        pltpu.make_async_copy(w_ref.at[p], out, sems.at[p])
        for p, out in enumerate((gw_out, uw_out, dw_out))
    ]
    copies.append(pltpu.make_async_copy(gi_ref, gi_out, sems.at[3]))
    for c in copies:
        c.start()
    row = rms_ref[0:1, :]
    lanes = lax.broadcasted_iota(jnp.int32, row.shape, 1)
    for p in range(3):
        rms_out[p] = jnp.sum(jnp.where(lanes == p, row, 0.0))
    for c in copies:
        c.wait()


def body(tokens, grad_out, w_gate, w_up, w_down):
    c = tokens.shape[1]
    h = w_gate.shape[0]
    vmem = pl.BlockSpec(memory_space=pltpu.VMEM)
    hbm = pl.BlockSpec(memory_space=pl.ANY)
    dma = pltpu.SemaphoreType.DMA
    grad_in, wgrads, rms = pl.pallas_call(
        kernel,
        out_shape=(
            pltpu.VMEM(tokens.shape, BF16),
            pltpu.VMEM((3, h, c), F32),
            pltpu.VMEM((8, 128), F32),
        ),
        in_specs=[hbm] * 5,
        out_specs=(vmem, hbm, vmem),
        scratch_shapes=[
            pltpu.VMEM((2, STEPS, 2, Y, 8, c), BF16),
            pltpu.VMEM((3, 256, c), BF16),
            pltpu.VMEM((128, c), BF16),
            pltpu.VMEM((128, c), BF16),
            pltpu.VMEM((STEPS, X, 16, 896), F32),
            pltpu.VMEM((STEPS, 3, 16, 896), BF16),
            pltpu.VMEM((STEPS, 3, 16, 896), BF16),
            pltpu.VMEM((STEPS, X, 16, 896), BF16),
            pltpu.VMEM((2, STEPS, 2, 64, c), BF16),
            pltpu.VMEM((STEPS, 2, 64, 512), BF16),
            pltpu.VMEM((STEPS, 64, 512), BF16),
            pltpu.VMEM((STEPS, 2, Y, 8, c), F32),
            pltpu.VMEM((STEPS, 3, 2, 8, c), BF16),
            pltpu.VMEM((STEPS, 3, 2, 8, c), BF16),
            pltpu.VMEM((STEPS, 2, 8, c), BF16),
            pltpu.VMEM((Z - 1, 8, c), BF16),
            pltpu.VMEM((8, c), F32),
            pltpu.VMEM((X * Y * 2, 8, 128), F32),
            pltpu.VMEM((Z, 8, 128), F32),
            pltpu.VMEM((2, 8, 128), F32),
            pltpu.VMEM((3, h, c), F32),
            dma, dma, dma((2,)), dma((3,)), dma((3,)), dma((3,)), dma((STEPS,)),
            dma((2, 3, CHUNKS)), dma((2, 3)), dma((4,)),
            dma((STEPS,)), dma((STEPS,)), dma((STEPS,)), dma((STEPS,)), dma, dma,
            dma((STEPS,)), dma, dma((STEPS,)), dma((2,)), dma((2,)), dma,
        ],
        compiler_params=pltpu.CompilerParams(
            collective_id=0, has_side_effects=True, vmem_limit_bytes=64_700_000
        ),
    )(tokens, grad_out, w_gate, w_up, w_down)
    wgrad = jax.ShapeDtypeStruct((h, c), F32)
    return pl.pallas_call(
        finish,
        out_shape=(
            jax.ShapeDtypeStruct(tokens.shape, BF16),
            wgrad,
            wgrad,
            wgrad,
            jax.ShapeDtypeStruct((3,), F32),
        ),
        in_specs=[hbm, hbm, vmem],
        out_specs=(hbm, hbm, hbm, hbm, pl.BlockSpec(memory_space=pltpu.SMEM)),
        scratch_shapes=[dma((4,))],
        compiler_params=pltpu.CompilerParams(vmem_limit_bytes=1024 * 1024),
    )(grad_in, wgrads, rms)


def solution(mesh):
    torus = Mesh(
        mesh.devices.reshape(mesh.shape["row"], mesh.shape["col"], 4, 2),
        ("row", "col", "depth_0", "depth_1"),
    )
    placed = P(ROW_DEPTH, "col")
    return jax.shard_map(
        body,
        mesh=torus,
        in_specs=(placed,) * 5,
        out_specs=(placed, placed, placed, placed, P()),
        check_vma=False,
    )
```

time: 77.3 us -> 72.8 us (0.942)
  Pallas kernels: 76.5 us -> 71.9 us
    pallas_call x1, Pallas kernels: 74.6 us -> 70 us  [body(): pl.pallas_call(kernel, out_shape=(pltpu.VMEM(tokens.shape, BF16), pltpu.V...]
where the time goes in v3:
time: 72.8 us; the launch traced here: 72.5 us
  Pallas kernels  71.9 us (99%)
    pallas_call x1, Pallas kernels, body(): pl.pallas_call(kernel, out_shape=(pltpu.VMEM(tokens.shape, BF16), pltpu.V...  70 us
    pallas_call x1, Pallas kernels, body(): pl.pallas_call(finish, out_shape=(jax.ShapeDtypeStruct(tokens.shape, BF16...  1.83 us

profile of v3, /device:TPU:1, one launch (start us, length us, event | category | flops | bytes accessed | tf_op | source)
XLA Modules:
  0.0 72.5 jit_solution(4404910335432535995)
XLA Ops:
  0.6 70.0 %shard_map.92 = (bf16[8,1152]{1,0:T(8,128)(2,1)S(1)}, f32[3,144,1152]{2,1,0:T(8,128)S(1)}, f32[8,128]{1,0:T(8,128)S(1)}) custom-call(bf16[8,1152]{1,0:T(8,128)(2,1)} %x_ref.1, bf16[8,1152]{1,0:T(8,128)(2,1)} %dy_ref.1, bf16[144,1152]{1,0:T(8,128)(2,1)} %wg_ref.1, bf16[144,1152]{1,0:T(8,128)(2,1)} %wu_ref.1, bf16[144,1152]{1,0:T(8,128)(2,1)} %wd_ref.1), custom_call_target="tpu_custom_call" | custom-call | tf_op jit(solution)/shard_map/pallas_call | solution.py:507
  70.7 1.8 %shard_map.93 = (bf16[8,1152]{1,0:T(8,128)(2,1)}, f32[144,1152]{1,0:T(8,128)}, f32[144,1152]{1,0:T(8,128)}, f32[144,1152]{1,0:T(8,128)}, f32[3]{0:T(128)}) custom-call(bf16[8,1152]{1,0:T(8,128)(2,1)S(1)} %get-tuple-element.8.gi_ref, f32[3,144,1152]{2,1,0:T(8,128)S(1)} %get-tuple-element.9.w_ref, f32[8,128]{1,0:T(8,128)S(1)} %get-tuple-element.10.rms_ref), custom_call_target="tpu_custom_call" | custom-call | tf_op jit(solution)/shard_map/pallas_call | solution.py:548

commit v4 on v3

--- a/solution.py
+++ b/solution.py
@@ -58,10 +58,10 @@
     x_ref, dy_ref, wg_ref, wu_ref, wd_ref,
     gi_out, w_out, rms_out,
     blk, wm, wlx, wld, pf, sx, rx, g, xs, ga, gb, gi, sy, ry, sz, rz, acc,
-    plane, line, sb, wacc,
-    feed, ysend, yrecv, wlocal, wsend, wrecv, send, frecv, urecv, vrecv,
+    plane, line, sb, wacc, own,
+    feed, hrecv, ysend, yrecv, wlocal, wsend, wrecv, send, frecv, urecv, vrecv,
     xgsend, xrecv, grecv, ryrecv, rzsend, rzrecv,
-    mxrecv, mgsend, mgrecv, nsend, nrecv, wsem,
+    precv, mgsend, mgrecv, nsend, nrecv, wsem,
 ):
     z = lax.axis_index("row")
     x = lax.axis_index("col")
@@ -91,6 +91,7 @@
     barrier = pltpu.get_barrier_semaphore()
     near = [zdev(1), zdev(Z - 1), mate]
     near += [xdev(o) for o in range(1, X)] + [ydev(o) for o in range(1, Y)]
+    near += [{**ydev(o), **mate} for o in range(1, Y)]
     for dev in near:
         pl.semaphore_signal(barrier, inc=1, device_id=dev, device_id_type=MESH)
 
@@ -111,25 +112,36 @@
             )
         )
     feeds = [
-        pltpu.make_async_copy(src, blk.at[0, 0, xd, y], feed)
+        pltpu.make_async_copy(src, own.at[xd], feed.at[0])
         for xd, src in ((0, x_ref), (1, dy_ref))
     ]
     for c in feeds + local:
         c.start()
+
+    @pl.when(k == 1)
+    def _():
+        for xd, src in ((0, x_ref), (1, dy_ref)):
+            pltpu.make_async_copy(src, blk.at[0, 0, 1, xd, y], feed.at[1]).start()
+
     wlx[64:128, :] = jnp.zeros((64, wlx.shape[1]), BF16)
     wld[0:64, :] = jnp.zeros((64, wld.shape[1]), BF16)
     wld[96:128, :] = jnp.zeros((32, wld.shape[1]), BF16)
-    wait_bytes(blk.at[0, 0, 0, 0:2], feed)
+    wait_bytes(own, feed.at[0])
+
+    @pl.when(k == 1)
+    def _():
+        wait_bytes(own, feed.at[1])
+
 
     with jax.named_scope("barrier"):
         pl.semaphore_wait(barrier, len(near))
 
     def chunk(direction, slot, q):
         at = ZL * max(q - 1, 0)
-        return blk.at[direction, slot, min(q, 1), :, :, at : at + ZL]
+        return blk.at[direction, slot, :, min(q, 1), :, :, at : at + ZL]
 
     def unit(direction, slot):
-        return blk.at[direction, slot, 0, y, :, ZL:]
+        return blk.at[direction, slot, :, 0, y, :, ZL:]
 
     def along(direction):
         return zdev(1) if direction == 0 else zdev(Z - 1)
@@ -152,12 +164,23 @@
             along(direction),
         )
 
-    unit_ring(0, 0, 0, 0, 1, 1).start()
-    unit_ring(1, 0, 0, 1, 1, 1).start()
+    def to_ring(o, xd, r):
+        rcopy(
+            own.at[xd],
+            blk.at[0, 0, k, xd, y],
+            ysend,
+            r,
+            {"depth_0": lax.rem(y + o, Y), "depth_1": 1},
+        ).start()
+
+    @pl.when(k == 0)
+    def _():
+        for xd in range(2):
+            to_ring(0, xd, hrecv)
+
     for o in (2, 1, 3):
         for xd in range(2):
-            own_unit = blk.at[0, 0, xd, y]
-            rcopy(own_unit, own_unit, ysend, yrecv.at[xd], ydev(o)).start()
+            to_ring(o, xd, yrecv.at[xd])
 
     def enter(q):
         ring(0, 0, 0, 0, 1, q, 1).start()
@@ -171,16 +194,6 @@
         rcopy(
             weights[p].at[128:144], tail.at[at + 16 : at + 32], wsend.at[p], wrecv.at[p], mate
         ).start()
-
-    wait_bytes(blk.at[0, 0, 0, 0:3], yrecv.at[0], "y")
-    enter(0)
-    wait_bytes(blk.at[0, 0, 1, 0:3], yrecv.at[1], "y")
-    for q in range(1, CHUNKS):
-        enter(q)
-
-    for p in range(3):
-        wait_bytes(wm.at[0, 0:144], wlocal.at[p], "w")
-        wait_bytes(wm.at[0, 0:144], wrecv.at[p], "w")
 
     def got(direction, slot, q, t, way):
         wait_bytes(chunk(direction, slot, q), frecv.at[way, lax.rem(t, 3), q], "ring")
@@ -244,17 +257,47 @@
     def wait_spread(t):
         @pl.when(t < STEPS)
         def _():
-            wait_bytes(blk.at[:, t, 0, 0:3, :, ZL:], vrecv.at[lax.rem(t, 4)], "spread")
+            wait_bytes(blk.at[:, t, :, 0, 0:3, :, ZL:], vrecv.at[lax.rem(t, 4)], "spread")
 
         @pl.when(t == STEPS)
         def _():
-            wait_bytes(blk.at[1, 0, 0, 0:3, :, ZL:], vrecv.at[lax.rem(t, 4)], "spread")
-
-    poll_unit(1)
-
-    def rows_of(t, xd):
+            wait_bytes(blk.at[1, 0, :, 0, 0:3, :, ZL:], vrecv.at[lax.rem(t, 4)], "spread")
+
+    @pl.when(k == 1)
+    def _():
+        wait_bytes(own, hrecv)
+        unit_ring(0, 0, 0, 0, 1, 1).start()
+        unit_ring(1, 0, 0, 1, 1, 1).start()
+        wait_bytes(blk.at[0, 0, :, 0, 0:3], yrecv.at[0], "y")
+        enter(0)
+        poll_unit(1)
+        wait_bytes(blk.at[0, 0, :, 1, 0:3], yrecv.at[1], "y")
+        for q in range(1, CHUNKS):
+            enter(q)
+
+    for p in range(3):
+        wait_bytes(wm.at[0, 0:144], wlocal.at[p], "w")
+        wait_bytes(wm.at[0, 0:144], wrecv.at[p], "w")
+
+    def rows_of(t, core, xd):
         slot = lax.rem(t, STEPS)
-        return blk[:, pl.ds(slot, 1), xd].astype(F32).reshape(64, -1).astype(BF16)
+        return blk[:, pl.ds(slot, 1), pl.ds(core, 1), xd].astype(F32).reshape(64, -1).astype(BF16)
+
+    def part_of(t, part):
+        slot = lax.rem(t, STEPS)
+        return blk.at[:, slot, 1] if part == 2 else blk.at[:, slot, 0, part]
+
+    def push(t, part):
+        ref = part_of(t, part)
+        rcopy(ref, ref, send.at[t - 1], precv.at[part, t - 1], {"depth_1": 0}).start()
+
+    def pushed(t, part):
+        wait_bytes(part_of(t, part), precv.at[part, t - 1], "push")
+
+    def stage_m(t):
+        pl.when(k == 0)(lambda: pushed(t, 2))
+        for xd in range(2):
+            xs[xd, pl.ds(t - 1, 1), 1] = rows_of(t, 1 - k, xd)[None]
 
     def put(i, value, at):
         pf[pl.ds(i, 1), :, :, at : at + value.shape[1]] = value.reshape(1, X, 16, -1)
@@ -351,7 +394,6 @@
             if p == 0:
                 for j in range(n):
                     wait_bytes(ga.at[first + j, 1], mgrecv.at[first + j], "mg")
-                    wait_bytes(xs.at[:, first + j, 1], mxrecv.at[first + j], "mx")
             gv = ga[pl.ds(first, n)].reshape(128 * n, 512)
             right = xs[p // 2, pl.ds(first, n)].reshape(128 * n, -1)
             news = [(p, 0, tn(gv[:, 128 * p : 128 * p + 128], right))]
@@ -372,22 +414,39 @@
 
     def step(t, carry):
         i = t - 1
-        poll(t, 0)
-        poll(t, 1)
-        pl.when(t < STEPS)(lambda: poll_unit(t + 1))
-        poll(t, 2)
+
+        @pl.when(k == 1)
+        def _():
+            poll(t, 0)
+            poll(t, 1)
+            pl.when(t < STEPS)(lambda: poll_unit(t + 1))
+            poll(t, 2)
+
         pl.when(t >= 3)(lambda: stage_b(t - 3))
+
+        @pl.when(k == 1)
+        def _():
+            wait_spread(t)
+            push(t, 0)
+
+        pl.when(k == 0)(lambda: pushed(t, 0))
         with jax.named_scope("a_x"):
-            wait_spread(t)
-            xv = rows_of(t, 0)
+            xv = rows_of(t, k, 0)
             xs[0, pl.ds(i, 1), 0] = xv[None]
             put(i, nt(xv, wm[0]), 0)
             put(i, nt(xv, wm[1]), 256)
             left = nt(xv, wlx[...])
-        poll(t, 3)
+
+        @pl.when(k == 1)
+        def _():
+            poll(t, 3)
+            push(t, 1)
+            push(t, 2)
+
         pl.when(t >= 5)(lambda: stage_c(t - 5))
+        pl.when(k == 0)(lambda: pushed(t, 1))
         with jax.named_scope("a_d"):
-            dv = rows_of(t, 1)
+            dv = rows_of(t, k, 1)
             xs[1, pl.ds(i, 1), 0] = dv[None]
             put(i, nt(dv, wm[2]), 512)
             put(i, left + nt(dv, wld[...]), 768)
@@ -397,10 +456,7 @@
                 rcopy(
                     sx.at[i, o - 1], rx.at[i, o - 1], xgsend.at[i], xrecv.at[i], xdev(o)
                 ).start()
-            for xd in range(2):
-                to_mate(
-                    xs.at[xd, i, 0], xs.at[xd, i, 1], send.at[i], mxrecv.at[i]
-                )
+        pl.when(t >= 2)(lambda: stage_m(t - 1))
         pl.when(t >= 7)(lambda: stage_d(t - 7))
         return carry
 
@@ -411,6 +467,7 @@
             wgrad(first, n, fresh, p)
 
     stage_c(4)
+    stage_m(STEPS)
     stage_d(2)
     stage_b(6)
     stage_c(5)
@@ -466,11 +523,22 @@
         total = total + rz[j].astype(F32)
     gi_out[...] = total.astype(BF16)
 
-    wait_bytes(wacc.at[0, 0:24], ysend)
     for p in range(3):
         wait_bytes(wm.at[0, 0:144], wsend.at[p])
+
+    @pl.when(k == 1)
+    def _():
+        wait_bytes(wacc.at[0, 0:24], ysend)
+        for i in range(STEPS):
+            wait_bytes(wacc.at[0:2, 0:144] if i < STEPS - 1 else wacc.at[0:3, 0:72], send.at[i])
+
+    @pl.when(k == 0)
+    def _():
+        wait_bytes(wacc.at[0, 0:32], ysend)
+        for i in range(STEPS):
+            wait_bytes(wacc.at[0, 0:32] if i < STEPS - 1 else wacc.at[0, 0:24], send.at[i])
+
     for i in range(STEPS):
-        wait_bytes(wacc.at[0:2, 0:80] if i < STEPS - 1 else wacc.at[0, 0:120], send.at[i])
         wait_bytes(pf.at[0, 0:3], xgsend.at[i])
     wait_bytes(ga.at[:, 0], mgsend)
     wait_bytes(sz.at[0, 1], rzsend)
@@ -514,7 +582,7 @@
         in_specs=[hbm] * 5,
         out_specs=(vmem, hbm, vmem),
         scratch_shapes=[
-            pltpu.VMEM((2, STEPS, 2, Y, 8, c), BF16),
+            pltpu.VMEM((2, STEPS, 2, 2, Y, 8, c), BF16),
             pltpu.VMEM((3, 256, c), BF16),
             pltpu.VMEM((128, c), BF16),
             pltpu.VMEM((128, c), BF16),
@@ -535,10 +603,11 @@
             pltpu.VMEM((Z, 8, 128), F32),
             pltpu.VMEM((2, 8, 128), F32),
             pltpu.VMEM((3, h, c), F32),
-            dma, dma, dma((2,)), dma((3,)), dma((3,)), dma((3,)), dma((STEPS,)),
+            pltpu.VMEM((2, 8, c), BF16),
+            dma((2,)), dma, dma, dma((2,)), dma((3,)), dma((3,)), dma((3,)), dma((STEPS,)),
             dma((2, 3, CHUNKS)), dma((2, 3)), dma((4,)),
             dma((STEPS,)), dma((STEPS,)), dma((STEPS,)), dma((STEPS,)), dma, dma,
-            dma((STEPS,)), dma, dma((STEPS,)), dma((2,)), dma((2,)), dma,
+            dma((3, STEPS)), dma, dma((STEPS,)), dma((2,)), dma((2,)), dma,
         ],
         compiler_params=pltpu.CompilerParams(
             collective_id=0, has_side_effects=True, vmem_limit_bytes=64_700_000

time: 72.8 us -> 71.3 us (0.979)
  Pallas kernels: 71.9 us -> 70.5 us
    pallas_call x1, Pallas kernels: 70 us -> 68.7 us  [body(): pl.pallas_call(kernel, out_shape=(pltpu.VMEM(tokens.shape, BF16), pltpu.V...]
where the time goes in v4:
time: 71.3 us; the launch traced here: 71.1 us
  Pallas kernels  70.5 us (99%)
    pallas_call x1, Pallas kernels, body(): pl.pallas_call(kernel, out_shape=(pltpu.VMEM(tokens.shape, BF16), pltpu.V...  68.7 us
    pallas_call x1, Pallas kernels, body(): pl.pallas_call(finish, out_shape=(jax.ShapeDtypeStruct(tokens.shape, BF16...  1.83 us

profile of v4, /device:TPU:1, one launch (start us, length us, event | category | flops | bytes accessed | tf_op | source)
XLA Modules:
  0.0 71.1 jit_solution(2808484852165771845)
XLA Ops:
  0.6 68.7 %shard_map.92 = (bf16[8,1152]{1,0:T(8,128)(2,1)S(1)}, f32[3,144,1152]{2,1,0:T(8,128)S(1)}, f32[8,128]{1,0:T(8,128)S(1)}) custom-call(bf16[8,1152]{1,0:T(8,128)(2,1)} %x_ref.1, bf16[8,1152]{1,0:T(8,128)(2,1)} %dy_ref.1, bf16[144,1152]{1,0:T(8,128)(2,1)} %wg_ref.1, bf16[144,1152]{1,0:T(8,128)(2,1)} %wu_ref.1, bf16[144,1152]{1,0:T(8,128)(2,1)} %wd_ref.1), custom_call_target="tpu_custom_call" | custom-call | tf_op jit(solution)/shard_map/pallas_call | solution.py:575
  69.3 1.8 %shard_map.93 = (bf16[8,1152]{1,0:T(8,128)(2,1)}, f32[144,1152]{1,0:T(8,128)}, f32[144,1152]{1,0:T(8,128)}, f32[144,1152]{1,0:T(8,128)}, f32[3]{0:T(128)}) custom-call(bf16[8,1152]{1,0:T(8,128)(2,1)S(1)} %get-tuple-element.8.gi_ref, f32[3,144,1152]{2,1,0:T(8,128)S(1)} %get-tuple-element.9.w_ref, f32[8,128]{1,0:T(8,128)S(1)} %get-tuple-element.10.rms_ref), custom_call_target="tpu_custom_call" | custom-call | tf_op jit(solution)/shard_map/pallas_call | solution.py:617

commit v5 on v4

--- a/solution.py
+++ b/solution.py
@@ -178,8 +178,8 @@
         for xd in range(2):
             to_ring(0, xd, hrecv)
 
-    for o in (2, 1, 3):
-        for xd in range(2):
+    for xd in range(2):
+        for o in (2, 1, 3):
             to_ring(o, xd, yrecv.at[xd])
 
     def enter(q):
@@ -479,8 +479,9 @@
     more(4, 2)
     stage_d(5)
     stage_c(7)
-    squares = {}
-    for p in range(3):
+    squares = wgrad(6, 2, False, 0)
+    stage_d(6)
+    for p in (1, 2):
         squares.update(wgrad(6, 2, False, p))
     value = jnp.zeros((8, 128), F32)
     for p in range(3):
@@ -506,7 +507,6 @@
                     ).start()
     wcopy = pltpu.make_async_copy(wacc, w_out, wsem)
     wcopy.start()
-    stage_d(6)
     stage_d(7, True)
     others = X * Y * 2 - 1
     wait_bytes(plane.at[0:others], nrecv.at[0], "plane")

time: 71.3 us -> 71.2 us (level)
  no operation moved by 1% of the time
where the time goes in v5:
time: 71.2 us; the launch traced here: 71 us
  Pallas kernels  70.4 us (99%)
    pallas_call x1, Pallas kernels, body(): pl.pallas_call(kernel, out_shape=(pltpu.VMEM(tokens.shape, BF16), pltpu.V...  68.5 us
    pallas_call x1, Pallas kernels, body(): pl.pallas_call(finish, out_shape=(jax.ShapeDtypeStruct(tokens.shape, BF16...  1.83 us

profile of v5, /device:TPU:1, one launch (start us, length us, event | category | flops | bytes accessed | tf_op | source)
XLA Modules:
  0.0 71.0 jit_solution(18194512560426812831)
XLA Ops:
  0.6 68.5 %shard_map.92 = (bf16[8,1152]{1,0:T(8,128)(2,1)S(1)}, f32[3,144,1152]{2,1,0:T(8,128)S(1)}, f32[8,128]{1,0:T(8,128)S(1)}) custom-call(bf16[8,1152]{1,0:T(8,128)(2,1)} %x_ref.1, bf16[8,1152]{1,0:T(8,128)(2,1)} %dy_ref.1, bf16[144,1152]{1,0:T(8,128)(2,1)} %wg_ref.1, bf16[144,1152]{1,0:T(8,128)(2,1)} %wu_ref.1, bf16[144,1152]{1,0:T(8,128)(2,1)} %wd_ref.1), custom_call_target="tpu_custom_call" | custom-call | tf_op jit(solution)/shard_map/pallas_call | solution.py:575
  69.2 1.8 %shard_map.93 = (bf16[8,1152]{1,0:T(8,128)(2,1)}, f32[144,1152]{1,0:T(8,128)}, f32[144,1152]{1,0:T(8,128)}, f32[144,1152]{1,0:T(8,128)}, f32[3]{0:T(128)}) custom-call(bf16[8,1152]{1,0:T(8,128)(2,1)S(1)} %get-tuple-element.8.gi_ref, f32[3,144,1152]{2,1,0:T(8,128)S(1)} %get-tuple-element.9.w_ref, f32[8,128]{1,0:T(8,128)S(1)} %get-tuple-element.10.rms_ref), custom_call_target="tpu_custom_call" | custom-call | tf_op jit(solution)/shard_map/pallas_call | solution.py:617
